TPU v7x, 8 devices: a whole 2x2x1 slice. The times are simulated.
8 devices in a mesh: dp: 1 (over z), a: 2 (over y), b: 4 (over x, core).
Axes of the slice: x: 2, y: 2, z: 1, core: 2. Of those that a mesh axis runs over, the one named last changes fastest.
Arguments:
- x: bfloat16 [2048, 8192], P('dp', ('a', 'b'))
- w_gate: bfloat16 [8192, 49152], P('a', 'b')
- w_up: bfloat16 [8192, 49152], P('a', 'b')
- w_down: bfloat16 [49152, 8192], P('b', 'a')
Outputs:
- output: bfloat16 [2048, 8192], P('dp', ('a', 'b'))
All inputs are finite; a program needn't handle non-finite values.
Results may differ from a plain program's by a relative error of at most 0.016.
Values are sent between devices in bfloat16 or wider.
A program may use at most 2 GiB of HBM per device.

v0:
```python
import jax
import jax.numpy as jnp


def solution(mesh):
    def step(x, w_gate, w_up, w_down):
        gate, up = jnp.dot(x, w_gate), jnp.dot(x, w_up)
        hidden = (jax.nn.silu(gate.astype(jnp.float32)) * up.astype(jnp.float32)).astype(jnp.bfloat16)
        return jnp.dot(hidden, w_down)

    return step
```

profile of v0, /device:TPU:0, one launch (start us, length us, event | category | flops | bytes accessed | tf_op | source)
XLA Modules:
  0.0 3103.5 jit_solution(1203452814323641750)
XLA Ops:
  6.5 0.0 all-gather.4.cloned.1.call-start
  6.5 0.7 all-gather.4.cloned.1.call-update
  7.3 0.0 all-reduce.7.cloned.1.call-start
  7.3 108.6 %all-gather.4.cloned.1.call-done = bf16[2048,4096]{1,0:T(8,128)(2,1)} async-done(((bf16[2048,1024]{1,0:T(8,128)(2,1)}), bf16[2048,4096]{1,0:T(8,128)(2,1)}) %all-gather.4.cloned.1.call-update) | async-done | bytes 16777232 | tf_op args[0]
  115.9 221.8 %fusion.9 = bf16[2048,12288]{1,0:T(8,128)(2,1)} fusion(bf16[2048,4096]{1,0:T(8,128)(2,1)} %all-gather.4.cloned.1.call-done, bf16[4096,12288]{1,0:T(8,128)(2,1)} %param.2), kind=kOutput, calls=%fused_computation.10 | convolution fusion | flops 206158430208 | bytes 167772160 | tf_op jit(solution)/dot_general | solution.py:7
  337.7 231.9 %fusion.8 = bf16[2048,12288]{1,0:T(8,128)(2,1)} fusion(bf16[2048,4096]{1,0:T(8,128)(2,1)} %all-gather.4.cloned.1.call-done, bf16[4096,12288]{1,0:T(8,128)(2,1)} %param.1), kind=kOutput, calls=%fused_computation.9 | convolution fusion | flops 206158430208 | bytes 167772160 | tf_op jit(solution)/dot_general | solution.py:7
  569.6 0.0 all-reduce.7.cloned.1.call-update
  569.7 0.0 reduce-scatter.4.cloned.1.call-start
  569.7 2174.2 %all-reduce.7.cloned.1.call-done = (bf16[2048,12288]{1,0:T(8,128)(2,1)}, bf16[2048,12288]{1,0:T(8,128)(2,1)}) async-done(((bf16[2048,12288]{1,0:T(8,128)(2,1)}, bf16[2048,12288]{1,0:T(8,128)(2,1)}), (bf16[2048,12288]{1,0:T(8,128)(2,1)}, bf16[2048,12288]{1,0:T(8,128)(2,1)})) %all-reduce.7.cloned.1.call-update) | async-done | bytes 100663312 | tf_op jit(solution)/dot_general | solution.py:7
  2743.9 231.5 %fusion.5 = bf16[2048,4096]{1,0:T(8,128)(2,1)} fusion(bf16[12288,4096]{1,0:T(8,128)(2,1)} %param.3, bf16[2048,12288]{1,0:T(8,128)(2,1)} %get-tuple-element.4, bf16[2048,12288]{1,0:T(8,128)(2,1)} %get-tuple-element.5), kind=kOutput, calls=%fused_computation.7 | convolution fusion | flops 206359756800 | bytes 218103808 | tf_op jit(solution)/dot_general | solution.py:9
  2975.4 0.0 reduce-scatter.4.cloned.1.call-update
  2975.4 121.2 %reduce-scatter.4.cloned.1.call-done = bf16[2048,1024]{1,0:T(8,128)(2,1)} async-done(((bf16[2048,4096]{1,0:T(8,128)(2,1)}), bf16[2048,1024]{1,0:T(8,128)(2,1)}) %reduce-scatter.4.cloned.1.call-update) | async-done | bytes 4194320
Async XLA Ops:
  6.5 109.4 %all-gather.4.cloned.1.call-start = ((), (), s32[]{:S(2)}) async-start(), calls=%async_computation.1 | async-start | bytes 20971520 | tf_op args[0]
  7.3 2736.6 %all-reduce.7.cloned.1.call-start = ((), (), s32[]{:S(2)}) async-start(), calls=%async_computation.3 | async-start | bytes 201326592 | tf_op jit(solution)/dot_general | solution.py:7
  569.7 2526.9 %reduce-scatter.4.cloned.1.call-start = ((), (), s32[]{:S(2)}) async-start(), calls=%async_computation.2 | async-start | bytes 20971520
Sparse Core Ops, SparseCore 0:
  8.9 107.0 all-gather.3
  569.8 2174.0 all-reduce.6
  2975.5 121.0 reduce-scatter.3
where the time goes:
time: 3110 us; the launch traced here: 3100 us
  waiting for transfers between devices  2400 us (77%)
  matrix products  685 us (22%)
    dot_general x1, waiting for transfers between devices, step(): gate, up = (jnp.dot(x, w_gate), jnp.dot(x, w_up))  2170 us
    dot_general x2, matrix products, step(): gate, up = (jnp.dot(x, w_gate), jnp.dot(x, w_up))  454 us
    dot_general x1, matrix products, step(): return jnp.dot(hidden, w_down)  231 us
    unnamed x5, waiting for transfers between devices  231 us
  transfers between devices with their start and end apart: 3, of which 3 were waited for; matrix products, arithmetic and copies ran while one was open for 0% of the time, Pallas kernels for 0%

commit v1 on v0

v1 whole, which is shorter than its diff:
```python
import functools

import jax
import jax.numpy as jnp
from jax import lax
from jax.experimental import pallas as pl
from jax.experimental.pallas import tpu as pltpu
from jax.sharding import PartitionSpec as P


HEAD = 128
HEAD_CUTS = (1024, 2048, 3072, 3072, 3072)
HEAD_GO = (3072, 3072, 2048, 2048, 1024, 1024)
BODY = (640, 256)
BODY_CUTS = (1024, 4352, 4352, 2560)
NB = 4

BF16, F32 = jnp.bfloat16, jnp.float32


MESH = pl.DeviceIdType.MESH


def places():
    me = lax.axis_index("b")
    return me, me + 1 - 2 * (me % 2), (me + 2) % NB


def greet(*others):
    barrier = pltpu.get_barrier_semaphore()
    for other in others:
        pl.semaphore_signal(barrier, inc=1, device_id={"b": other}, device_id_type=MESH)
    pl.semaphore_wait(barrier, len(others))


def remote(src, dst, send, recv, k, to):
    return pltpu.make_async_remote_copy(
        src_ref=src, dst_ref=dst, send_sem=send.at[k], recv_sem=recv.at[k],
        device_id={"b": to}, device_id_type=MESH,
    )


def block(i, cols):
    return pl.ds(pl.multiple_of(i * cols, cols), cols)


STEP = 256


def steps(n):
    return [slice(o, o + STEP) for o in range(0, n, STEP)]


def head_kernel(
    base, half, x_ref, wg_ref, wu_ref, g_ref, u_ref, o_ref, rb_ref, ro_ref,
    xs, ws, acc, stage, send, recv, local, wsem, ssem, tsem, osem,
):
    me, mate, far = places()
    order = (me, mate, far, (mate + 2) % NB)
    a = lax.axis_index("a")
    rows, cols, n = xs.shape[1], xs.shape[2], g_ref.shape[1]
    src = x_ref.at[pl.ds(pl.multiple_of(rows * (1 - a), rows), rows), :]
    own = pltpu.make_async_copy(src, xs.at[0], local)
    own.start()
    weights = []
    for i, blk in enumerate(order):
        at = pl.ds(pl.multiple_of(blk * cols, cols), cols)
        for j, w in enumerate((wg_ref, wu_ref)):
            k = 2 * i + j
            weights.append(pltpu.make_async_copy(w.at[at, pl.ds(0, n)], ws.at[k], wsem.at[k]))
    weights[0].start()
    weights[1].start()
    greet(mate, far)
    across = remote(src, xs.at[2], send, recv, 0, far)
    beside = remote(src, xs.at[1], send, recv, 1, mate)
    across.start()
    beside.start()
    for w in weights[2:]:
        w.start()
    pieces = (
        (base + half * (1 - a), rb_ref, 0, half),
        (rows * a, ro_ref, 0, rows),
        (base + half * a, ro_ref, rows, half),
    )
    ins, outs, o = [], [], 0
    for k, (at, dst, to, m) in enumerate(pieces):
        mid = stage.at[pl.ds(o, m), :]
        ins.append(
            pltpu.make_async_copy(x_ref.at[pl.ds(pl.multiple_of(at, rows), m), :], mid, ssem.at[k])
        )
        outs.append(pltpu.make_async_copy(mid, dst.at[pl.ds(to, m), :], tsem.at[k]))
        o += m
    for c in ins:
        c.start()

    def product(i):
        for j, o_bf in enumerate((g_ref, u_ref)):
            weights[2 * i + j].wait()
            for at in steps(n):
                t = jnp.dot(xs[i], ws[2 * i + j, :, at], preferred_element_type=F32)
                if i:
                    t = t + acc[j, :, at]
                if i < NB - 1:
                    acc[j, :, at] = t
                else:
                    o_bf[:, at] = t.astype(BF16)

    own.wait()
    product(0)
    beside.wait_recv()
    product(1)
    for c, d in zip(ins, outs):
        c.wait()
        d.start()
    across.wait_recv()
    relay = remote(xs.at[2], xs.at[3], send, recv, 2, mate)
    relay.start()
    product(2)
    relay.wait_recv()
    keeps = [
        pltpu.make_async_copy(xs.at[i], o_ref.at[:, block(blk, cols)], osem.at[i])
        for i, blk in enumerate(order)
    ]
    for c in keeps:
        c.start()
    product(3)
    for c in keeps + outs:
        c.wait()
    across.wait_send()
    beside.wait_send()
    relay.wait_send()


def gather_head(x, wg, wu, base, half, n):
    cols = x.shape[1]
    hbm, vmem = pl.BlockSpec(memory_space=pl.ANY), pl.BlockSpec(memory_space=pltpu.VMEM)
    shape = lambda *dims: jax.ShapeDtypeStruct(dims, BF16)
    dma = pltpu.SemaphoreType.DMA
    return pl.pallas_call(
        functools.partial(head_kernel, base, half),
        out_shape=(
            shape(HEAD, n), shape(HEAD, n), shape(HEAD, NB * cols),
            shape(half, cols), shape(HEAD + half, cols),
        ),
        in_specs=[hbm, hbm, hbm],
        out_specs=(vmem, vmem, hbm, hbm, hbm),
        scratch_shapes=[
            pltpu.VMEM((NB, HEAD, cols), BF16),
            pltpu.VMEM((2 * NB, cols, n), BF16),
            pltpu.VMEM((2, HEAD, n), F32),
            pltpu.VMEM((HEAD + 2 * half, cols), BF16),
            dma((3,)), dma((3,)), dma, dma((2 * NB,)), dma((3,)), dma((3,)), dma((NB,)),
        ],
        compiler_params=pltpu.CompilerParams(
            collective_id=0, has_side_effects=True, vmem_limit_bytes=60 << 20
        ),
        name="gather_head",
    )(x, wg, wu)


def tail_kernel(
    y_ref, h_ref, w_ref, o_ref, hb, ws, out, got, mid, send, recv, hsem, wsem
):
    me, mate, far = places()
    cols = o_ref.shape[1]
    depth = hb.shape[1]
    order = ((mate + 2) % NB, mate, far, me)
    here = pltpu.make_async_copy(h_ref, hb, hsem)
    here.start()
    weights = []
    for i, blk in enumerate(order):
        src = w_ref.at[pl.ds(w_ref.shape[0] - depth, depth), block(blk, cols)]
        weights.append(pltpu.make_async_copy(src, ws.at[i], wsem.at[i]))
        weights[-1].start()
    greet(mate, far)
    here.wait()

    def term(i, dst):
        weights[i].wait()
        for at in steps(cols):
            y = y_ref[:, pl.ds(pl.multiple_of(order[i] * cols + at.start, STEP), STEP)]
            y = y + jnp.dot(hb[...], ws[i, :, at], preferred_element_type=F32)
            dst[:, at] = y.astype(dst.dtype)

    first = [remote(out.at[k], got.at[k], send, recv, k, mate) for k in range(2)]
    for k in range(2):
        term(k, out.at[k])
        first[k].start()
    term(2, mid)
    first[0].wait_recv()
    out[2] = (mid[...] + got[0].astype(F32)).astype(BF16)
    last = remote(out.at[2], got.at[2], send, recv, 2, far)
    last.start()
    term(3, mid)
    first[1].wait_recv()
    last.wait_recv()
    o_ref[...] = (mid[...] + got[1].astype(F32) + got[2].astype(F32)).astype(BF16)
    for c in first:
        c.wait_send()
    last.wait_send()


def scatter_head(y, h, wd):
    rows, cols, depth = y.shape[0], y.shape[1] // NB, h.shape[1]
    hbm, vmem = pl.BlockSpec(memory_space=pl.ANY), pl.BlockSpec(memory_space=pltpu.VMEM)
    dma = pltpu.SemaphoreType.DMA
    return pl.pallas_call(
        tail_kernel,
        out_shape=jax.ShapeDtypeStruct((rows, cols), BF16),
        in_specs=[vmem, hbm, hbm],
        out_specs=vmem,
        scratch_shapes=[
            pltpu.VMEM((rows, depth), BF16),
            pltpu.VMEM((NB, depth, cols), BF16),
            pltpu.VMEM((3, rows, cols), BF16),
            pltpu.VMEM((3, rows, cols), BF16),
            pltpu.VMEM((rows, cols), F32),
            dma((3,)), dma((3,)), dma, dma((NB,)),
        ],
        compiler_params=pltpu.CompilerParams(
            collective_id=1, has_side_effects=True, vmem_limit_bytes=20 << 20
        ),
        name="scatter_head",
    )(y, h, wd)


def f32dot(l, r):
    return jnp.dot(l, r, preferred_element_type=F32)


def spans(cuts):
    out, o = [], 0
    for c in cuts:
        out.append((o, o + c))
        o += c
    return out


def body(x, wg, wu, wd):
    a, b = lax.axis_index("a"), lax.axis_index("b")
    cols = x.shape[1]
    half = x.shape[0] // 2 - HEAD
    swap = lambda v: lax.ppermute(v, "a", [(0, 1), (1, 0)])
    col = lambda v, s: lax.slice_in_dim(v, s[0], s[1], axis=1)
    row = lambda v, s: lax.slice_in_dim(v, s[0], s[1], axis=0)
    fence = lax.optimization_barrier
    nexts = [lax.rem(b + k, NB) * cols for k in range(NB)]

    def shift(v, k):
        return lax.ppermute(v, "b", [(i, (i + k) % NB) for i in range(NB)])

    def gather(rows):
        full = jnp.zeros((rows.shape[0], NB * cols), BF16)
        full = lax.dynamic_update_slice(full, rows, (0, nexts[0]))
        for k in (1, 2, 3):
            got = shift(rows, k)
            full = lax.dynamic_update_slice(full, got, (0, nexts[NB - k]))
        return full

    def scatter(y):
        total = lax.dynamic_slice_in_dim(y, nexts[0], cols, 1)
        for k in (1, 2, 3):
            out = lax.dynamic_slice_in_dim(y, nexts[k], cols, 1).astype(BF16)
            total = total + shift(out, k).astype(F32)
        return total.astype(BF16)

    base = 2 * HEAD
    head_spans, body_spans = spans(HEAD_CUTS), spans(BODY_CUTS)

    g0, u0, xh, body_rows, own_rows = gather_head(x, wg, wu, base, half, HEAD_CUTS[0])
    part = lambda xs, w, s: f32dot(xs, col(w, s)).astype(BF16)

    def swaps(g, u):
        return swap(g), swap(u)

    def parts(xs, s):
        g = part(xs, wg, s)
        return swaps(g, part(xs, wu, s))

    head_parts = [swaps(g0, u0)]
    head_parts += [parts(xh, s) for i, s in enumerate(head_spans) if i]
    x_other = gather(body_rows)
    x_own = gather(own_rows)
    body_parts = [parts(x_other, s) for s in body_spans]

    def hidden(xs, s, rg, ru):
        g = f32dot(xs, col(wg, s))
        u = f32dot(xs, col(wu, s)) + ru.astype(F32)
        return (jax.nn.silu(g + rg.astype(F32)) * u).astype(BF16)

    head_hid = [hidden(x_own[:HEAD], s, *head_parts[i]) for i, s in enumerate(head_spans)]
    head_hid = jnp.concatenate(lax.optimization_barrier(head_hid), 1)
    go_spans = spans(HEAD_GO)
    head_got = [swap(col(head_hid, s)) for s in go_spans]

    offs = spans(BODY)
    body_hid = [[] for _ in BODY]
    body_got = [[] for _ in BODY]
    for i, s in enumerate(body_spans):
        for j, o in enumerate(offs):
            xs = x_own[HEAD + o[0] : HEAD + o[1]]
            rg, ru = (row(v, o) for v in body_parts[i])
            h = hidden(xs, s, rg, ru)
            body_hid[j].append(h)
            body_got[j].append(swap(h))

    out = jnp.zeros((x.shape[0], cols), BF16)
    h = jnp.concatenate([head_hid] + [jnp.concatenate(v, 1) for v in body_hid])
    r = scatter(f32dot(h, wd))
    out = lax.dynamic_update_slice(out, r[:HEAD], (HEAD * a, 0))
    out = lax.dynamic_update_slice(out, r[HEAD:], (base + half * a, 0))

    def down(got, cuts, i):
        return f32dot(got[i], row(wd, cuts[i]))

    for j, o in enumerate(offs):
        n = len(body_spans)
        terms = fence([down(body_got[j], body_spans, i) for i in range(n - 1)])
        y = f32dot(body_got[j][-1], row(wd, body_spans[-1]))
        for t in terms:
            y = y + t
        at = base + half * (1 - a) + o[0]
        r = scatter(y)
        out = lax.dynamic_update_slice(out, r, (at, 0))

    y = down(head_got, go_spans, 0)
    for i in range(1, len(go_spans) - 1):
        y = fence(y) + down(head_got, go_spans, i)
    out, y = fence((out, y))
    r = scatter_head(y, head_got[-1], wd)
    return lax.dynamic_update_slice(out, r, (HEAD * (1 - a), 0))


def solution(mesh):
    return jax.shard_map(
        body,
        mesh=mesh,
        in_specs=(P("dp", ("a", "b")), P("a", "b"), P("a", "b"), P("b", "a")),
        out_specs=P("dp", ("a", "b")),
        check_vma=False,
    )
```

time: 3110 us -> 2420 us (0.78)
  waiting for transfers between devices: 2400 us -> 1210 us
  matrix products: 685 us -> 1060 us
  local copies, waits for them, and re-layouts: 0 us -> 46.1 us
  starting transfers between devices: 0.08 us -> 45.5 us
    dot_general x1 -> x0, waiting for transfers between devices: 2170 us -> none  [step(): gate, up = (jnp.dot(x, w_gate), jnp.dot(x, w_up))]
    ppermute x0 -> x47, waiting for transfers between devices: none -> 1210 us  [the longest x32 1090 us: body(): swap = lambda v: lax.ppermute(v, 'a', [(0, 1), (1, 0)])]
    dot_general x3 -> x56, matrix products: 685 us -> 1060 us  [f32dot(): return jnp.dot(l, r, preferred_element_type=F32)]
    unnamed x5 -> x0, waiting for transfers between devices: 231 us -> none
    ppermute x0 -> x47, starting transfers between devices: none -> 45.5 us  [the longest x32 33.7 us: body(): swap = lambda v: lax.ppermute(v, 'a', [(0, 1), (1, 0)])]
  transfers between devices with their start and end apart: 3 -> 47, of which waited for: 3 -> 19; matrix products, arithmetic and copies ran while one was open for 0% -> 47% of each run, Pallas kernels for 0% -> 0%
where the time goes in v1:
time: 2420 us
  waiting for transfers between devices  1210 us (50%)
  matrix products  1060 us (44%)
  local copies, waits for them, and re-layouts  46.1 us (2%)
  starting transfers between devices  45.5 us (2%)
  other arithmetic  27.3 us (1%)
  Pallas kernels  24.2 us (1%)
    ppermute x32, waiting for transfers between devices, body(): swap = lambda v: lax.ppermute(v, 'a', [(0, 1), (1, 0)])  1090 us
    dot_general x56, matrix products, f32dot(): return jnp.dot(l, r, preferred_element_type=F32)  1060 us
    ppermute x15, waiting for transfers between devices, shift(): return lax.ppermute(v, 'b', [(i, (i + k) % NB) for i in range(NB)])  121 us
  transfers between devices with their start and end apart: 47, of which 19 were waited for; matrix products, arithmetic and copies ran while one was open for 47% of the time, Pallas kernels for 0%

profile of v1, /device:TPU:0, one launch (start us, length us, event | category | flops | bytes accessed | tf_op | source)
XLA Modules:
  0.0 2416.5 jit_solution(1928300653344956138)
XLA Ops:
  120.5 23.0 fusion.156
  143.5 22.9 fusion.159
  166.5 39.4 %fusion.112 = bf16[896,4352]{1,0:T(8,128)(2,1)} fusion(bf16[896,4096]{1,0:T(8,128)(2,1)S(1)} %constant_dynamic-update-slice_fusion.6, bf16[4096,12288]{1,0:T(8,128)(2,1)} %wg_ref.1), kind=kOutput, calls=%fused_computation.111 | convolution fusion | flops 31947718656 | bytes 50790400 | tf_op jit(solution)/shard_map/dot_general | solution.py:228
  205.9 39.0 %fusion.115 = bf16[896,4352]{1,0:T(8,128)(2,1)} fusion(bf16[896,4096]{1,0:T(8,128)(2,1)S(1)} %constant_dynamic-update-slice_fusion.6, bf16[4096,12288]{1,0:T(8,128)(2,1)} %wu_ref.1), kind=kOutput, calls=%fused_computation.112 | convolution fusion | flops 31947718656 | bytes 50790400 | tf_op jit(solution)/shard_map/dot_general | solution.py:228
  244.9 39.2 %fusion.106 = bf16[896,4352]{1,0:T(8,128)(2,1)} fusion(bf16[896,4096]{1,0:T(8,128)(2,1)S(1)} %constant_dynamic-update-slice_fusion.6, bf16[4096,12288]{1,0:T(8,128)(2,1)} %wg_ref.1), kind=kOutput, calls=%fused_computation.109 | convolution fusion | flops 31947718656 | bytes 50790400 | tf_op jit(solution)/shard_map/dot_general | solution.py:228
  284.1 39.0 %fusion.109 = bf16[896,4352]{1,0:T(8,128)(2,1)} fusion(bf16[896,4096]{1,0:T(8,128)(2,1)S(1)} %constant_dynamic-update-slice_fusion.6, bf16[4096,12288]{1,0:T(8,128)(2,1)} %wu_ref.1), kind=kOutput, calls=%fused_computation.110 | convolution fusion | flops 31947718656 | bytes 50790400 | tf_op jit(solution)/shard_map/dot_general | solution.py:228
  358.2 30.8 %fusion.18 = f32[640,4352]{1,0:T(8,128)} fusion(bf16[4096,12288]{1,0:T(8,128)(2,1)} %wg_ref.1, bf16[1024,4096]{1,0:T(8,128)(2,1)} %constant_dynamic-update-slice_fusion.10), kind=kOutput, calls=%fused_computation.18 | convolution fusion | flops 22817013760 | bytes 52035584 | tf_op jit(solution)/shard_map/dot_general | solution.py:228
  389.1 30.9 %fusion.30 = f32[640,4352]{1,0:T(8,128)} fusion(bf16[4096,12288]{1,0:T(8,128)(2,1)} %wg_ref.1, bf16[1024,4096]{1,0:T(8,128)(2,1)} %constant_dynamic-update-slice_fusion.10), kind=kOutput, calls=%fused_computation.30 | convolution fusion | flops 22817013760 | bytes 52035584 | tf_op jit(solution)/shard_map/dot_general | solution.py:228
  419.9 21.7 fusion.96
  579.5 363.2 %collective-permute-done.45 = bf16[128,1024]{1,0:T(8,128)(2,1)S(1)} collective-permute-done((bf16[128,1024]{1,0:T(8,128)(2,1)S(1)}, bf16[128,1024]{1,0:T(8,128)(2,1)S(1)}, u32[]{:S(2)}, u32[]{:S(2)}) %collective-permute-start.45) | collective-permute-done | bytes 262176 | tf_op jit(solution)/shard_map/ppermute | solution.py:243
  1002.9 30.9 %collective-permute-done.17 = bf16[896,1024]{1,0:T(8,128)(2,1)} collective-permute-done((bf16[896,1024]{1,0:T(8,128)(2,1)S(1)}, bf16[896,1024]{1,0:T(8,128)(2,1)}, u32[]{:S(2)}, u32[]{:S(2)}) %collective-permute-start.17) | collective-permute-done | bytes 1835040 | tf_op jit(solution)/shard_map/ppermute | solution.py:243
  1110.1 24.4 %multiply_convert_fusion.2 = bf16[640,2560]{1,0:T(8,128)(2,1)} fusion(f32[640,2560]{1,0:T(8,128)} %fusion.96, bf16[4096,12288]{1,0:T(8,128)(2,1)} %wu_ref.1, bf16[896,2560]{1,0:T(8,128)(2,1)} %collective-permute-done.23, bf16[896,2560]{1,0:T(8,128)(2,1)} %collective-permute-done.22, bf16[1024,4096]{1,0:T(8,128)(2,1)} %constant_dynamic-update-slice_fusion.10), kind=kOutput, calls=%fused_computation.123 | convolution fusion | flops 13438156800 | bytes 42598400 | tf_op jit(solution)/shard_map/dot_general | solution.py:228
  1157.8 267.4 %collective-permute-done.18 = bf16[896,4352]{1,0:T(8,128)(2,1)} collective-permute-done((bf16[896,4352]{1,0:T(8,128)(2,1)}, bf16[896,4352]{1,0:T(8,128)(2,1)}, u32[]{:S(2)}, u32[]{:S(2)}) %collective-permute-start.18) | collective-permute-done | bytes 7798816 | tf_op jit(solution)/shard_map/ppermute | solution.py:243
  1446.5 145.8 %collective-permute-done.19 = bf16[896,4352]{1,0:T(8,128)(2,1)} collective-permute-done((bf16[896,4352]{1,0:T(8,128)(2,1)}, bf16[896,4352]{1,0:T(8,128)(2,1)}, u32[]{:S(2)}, u32[]{:S(2)}) %collective-permute-start.19) | collective-permute-done | bytes 7798816 | tf_op jit(solution)/shard_map/ppermute | solution.py:243
  1652.7 37.6 %multiply_convert_fusion = bf16[640,4352]{1,0:T(8,128)(2,1)} fusion(f32[640,4352]{1,0:T(8,128)} %fusion.18, bf16[4096,12288]{1,0:T(8,128)(2,1)} %wu_ref.1, bf16[896,4352]{1,0:T(8,128)(2,1)} %collective-permute-done.21, bf16[896,4352]{1,0:T(8,128)(2,1)} %collective-permute-done.20, bf16[1024,4096]{1,0:T(8,128)(2,1)} %constant_dynamic-update-slice_fusion.10), kind=kOutput, calls=%fused_computation.106 | convolution fusion | flops 22844866560 | bytes 68747264 | tf_op jit(solution)/shard_map/dot_general | solution.py:228
  1690.3 37.2 %multiply_convert_fusion.1 = bf16[640,4352]{1,0:T(8,128)(2,1)} fusion(f32[640,4352]{1,0:T(8,128)} %fusion.30, bf16[4096,12288]{1,0:T(8,128)(2,1)} %wu_ref.1, bf16[896,4352]{1,0:T(8,128)(2,1)} %collective-permute-done.19, bf16[896,4352]{1,0:T(8,128)(2,1)} %collective-permute-done.18, bf16[1024,4096]{1,0:T(8,128)(2,1)} %constant_dynamic-update-slice_fusion.10), kind=kOutput, calls=%fused_computation.107 | convolution fusion | flops 22844866560 | bytes 68747264 | tf_op jit(solution)/shard_map/dot_general | solution.py:228
  1727.5 149.2 %fusion.32 = f32[1024,4096]{1,0:T(8,128)} fusion(bf16[12288,4096]{1,0:T(8,128)(2,1)} %w_ref.1, bf16[256,2560]{1,0:T(8,128)(2,1)} %multiply_convert_fusion.5, bf16[256,4352]{1,0:T(8,128)(2,1)} %multiply_convert_fusion.3, bf16[256,4352]{1,0:T(8,128)(2,1)} %multiply_convert_fusion.4, bf16[256,1024]{1,0:T(8,128)(2,1)} %multiply_convert_fusion.10, ...), kind=kOutput, calls=%fused_computation.32 | convolution fusion | flops 103305707520 | bytes 142606336 | tf_op jit(solution)/shard_map/dot_general | solution.py:228
  1885.1 21.2 fusion.80
  1906.3 24.2 %collective-permute-done.26 = bf16[1024,1024]{1,0:T(8,128)(2,1)S(1)} collective-permute-done((bf16[1024,1024]{1,0:T(8,128)(2,1)}, bf16[1024,1024]{1,0:T(8,128)(2,1)S(1)}, u32[]{:S(2)}, u32[]{:S(2)}) %collective-permute-start.26) | collective-permute-done | bytes 2097184 | tf_op jit(solution)/shard_map/ppermute | solution.py:250
  1930.5 45.0 %collective-permute-done.25 = bf16[1024,1024]{1,0:T(8,128)(2,1)S(1)} collective-permute-done((bf16[1024,1024]{1,0:T(8,128)(2,1)}, bf16[1024,1024]{1,0:T(8,128)(2,1)S(1)}, u32[]{:S(2)}, u32[]{:S(2)}) %collective-permute-start.25) | collective-permute-done | bytes 2097184 | tf_op jit(solution)/shard_map/ppermute | solution.py:250
  2003.7 217.2 %collective-permute-done.37 = bf16[256,4352]{1,0:T(8,128)(2,1)} collective-permute-done((bf16[256,4352]{1,0:T(8,128)(2,1)}, bf16[256,4352]{1,0:T(8,128)(2,1)}, u32[]{:S(2)}, u32[]{:S(2)}) %collective-permute-start.37) | collective-permute-done | bytes 2228256 | tf_op jit(solution)/shard_map/ppermute | solution.py:243
  2238.7 30.5 %fusion.6 = f32[640,4096]{1,0:T(8,128)} fusion(bf16[640,4352]{1,0:T(8,128)(2,1)} %collective-permute-done.29, bf16[12288,4096]{1,0:T(8,128)(2,1)} %w_ref.1), kind=kOutput, calls=%fused_computation.6 | convolution fusion | flops 22817013760 | bytes 51707904 | tf_op jit(solution)/shard_map/dot_general | solution.py:228
  2269.2 30.4 %fusion.2 = f32[640,4096]{1,0:T(8,128)} fusion(bf16[640,4352]{1,0:T(8,128)(2,1)} %collective-permute-done.30, bf16[12288,4096]{1,0:T(8,128)(2,1)} %w_ref.1), kind=kOutput, calls=%fused_computation.2 | convolution fusion | flops 22817013760 | bytes 51707904 | tf_op jit(solution)/shard_map/dot_general | solution.py:228
  2353.4 26.6 %collective-permute-done.32 = bf16[640,1024]{1,0:T(8,128)(2,1)} collective-permute-done((bf16[640,1024]{1,0:T(8,128)(2,1)}, bf16[640,1024]{1,0:T(8,128)(2,1)}, u32[]{:S(2)}, u32[]{:S(2)}) %collective-permute-start.32) | collective-permute-done | bytes 1310752 | tf_op jit(solution)/shard_map/ppermute | solution.py:250
  (195 shorter events, 678.6 us)
Async XLA Ops:
  13.5 98.3 %collective-permute-start.13 = (bf16[896,1024]{1,0:T(8,128)(2,1)}, bf16[896,1024]{1,0:T(8,128)(2,1)}, u32[]{:S(2)}, u32[]{:S(2)}) collective-permute-start(bf16[896,1024]{1,0:T(8,128)(2,1)} %get-tuple-element.32), channel_id=1, source_target_pairs={{0,1},{1,2},{2,3},{3,0},{4,5},{5,6},{6,7},{7,4}} | collective-permute-start | bytes 5505032 | tf_op jit(solution)/shard_map/ppermute | solution.py:250
  14.1 100.8 %collective-permute-start.14 = (bf16[896,1024]{1,0:T(8,128)(2,1)}, bf16[896,1024]{1,0:T(8,128)(2,1)}, u32[]{:S(2)}, u32[]{:S(2)}) collective-permute-start(bf16[896,1024]{1,0:T(8,128)(2,1)} %get-tuple-element.32), channel_id=1, source_target_pairs={{0,2},{1,3},{2,0},{3,1},{4,6},{5,7},{6,4},{7,5}} | collective-permute-start | bytes 5505032 | tf_op jit(solution)/shard_map/ppermute | solution.py:250
  15.2 102.8 %collective-permute-start.15 = (bf16[896,1024]{1,0:T(8,128)(2,1)}, bf16[896,1024]{1,0:T(8,128)(2,1)}, u32[]{:S(2)}, u32[]{:S(2)}) collective-permute-start(bf16[896,1024]{1,0:T(8,128)(2,1)} %get-tuple-element.32), channel_id=1, source_target_pairs={{0,3},{1,0},{2,1},{3,2},{4,7},{5,4},{6,5},{7,6}} | collective-permute-start | bytes 5505032 | tf_op jit(solution)/shard_map/ppermute | solution.py:250
  15.9 329.6 %collective-permute-start = (bf16[1024,1024]{1,0:T(8,128)(2,1)}, bf16[1024,1024]{1,0:T(8,128)(2,1)}, u32[]{:S(2)}, u32[]{:S(2)}) collective-permute-start(bf16[1024,1024]{1,0:T(8,128)(2,1)} %get-tuple-element.23), channel_id=1, source_target_pairs={{0,1},{1,2},{2,3},{3,0},{4,5},{5,6},{6,7},{7,4}} | collective-permute-start | bytes 6291464 | tf_op jit(solution)/shard_map/ppermute | solution.py:250
  15.9 334.0 %collective-permute-start.1 = (bf16[1024,1024]{1,0:T(8,128)(2,1)}, bf16[1024,1024]{1,0:T(8,128)(2,1)}, u32[]{:S(2)}, u32[]{:S(2)}) collective-permute-start(bf16[1024,1024]{1,0:T(8,128)(2,1)} %get-tuple-element.23), channel_id=1, source_target_pairs={{0,2},{1,3},{2,0},{3,1},{4,6},{5,7},{6,4},{7,5}} | collective-permute-start | bytes 6291464 | tf_op jit(solution)/shard_map/ppermute | solution.py:250
  111.8 242.0 %collective-permute-start.2 = (bf16[1024,1024]{1,0:T(8,128)(2,1)}, bf16[1024,1024]{1,0:T(8,128)(2,1)}, u32[]{:S(2)}, u32[]{:S(2)}) collective-permute-start(bf16[1024,1024]{1,0:T(8,128)(2,1)} %get-tuple-element.23), channel_id=1, source_target_pairs={{0,3},{1,0},{2,1},{3,2},{4,7},{5,4},{6,5},{7,6}} | collective-permute-start | bytes 6291464 | tf_op jit(solution)/shard_map/ppermute | solution.py:250
  115.0 439.2 %collective-permute-start.3 = (bf16[128,1024]{1,0:T(8,128)(2,1)}, bf16[128,1024]{1,0:T(8,128)(2,1)}, u32[]{:S(2)}, u32[]{:S(2)}) collective-permute-start(bf16[128,1024]{1,0:T(8,128)(2,1)} %get-tuple-element.24), channel_id=1, source_target_pairs={{0,4},{4,0},{1,5},{5,1},{2,6},{6,2},{3,7},{7,3}} | collective-permute-start | bytes 786440 | tf_op jit(solution)/shard_map/ppermute | solution.py:243
  118.0 442.5 %collective-permute-start.4 = (bf16[128,1024]{1,0:T(8,128)(2,1)}, bf16[128,1024]{1,0:T(8,128)(2,1)}, u32[]{:S(2)}, u32[]{:S(2)}) collective-permute-start(bf16[128,1024]{1,0:T(8,128)(2,1)} %get-tuple-element.25), channel_id=1, source_target_pairs={{0,4},{4,0},{1,5},{5,1},{2,6},{6,2},{3,7},{7,3}} | collective-permute-start | bytes 786440 | tf_op jit(solution)/shard_map/ppermute | solution.py:243
  345.4 189.0 %collective-permute-start.5 = (bf16[128,2048]{1,0:T(8,128)(2,1)}, bf16[128,2048]{1,0:T(8,128)(2,1)}, u32[]{:S(2)}, u32[]{:S(2)}) collective-permute-start(bf16[128,2048]{1,0:T(8,128)(2,1)} %fusion.221), channel_id=1, source_target_pairs={{0,4},{4,0},{1,5},{5,1},{2,6},{6,2},{3,7},{7,3}} | collective-permute-start | bytes 1572872 | tf_op jit(solution)/shard_map/ppermute | solution.py:243
  349.9 194.6 %collective-permute-start.6 = (bf16[128,2048]{1,0:T(8,128)(2,1)}, bf16[128,2048]{1,0:T(8,128)(2,1)}, u32[]{:S(2)}, u32[]{:S(2)}) collective-permute-start(bf16[128,2048]{1,0:T(8,128)(2,1)} %fusion.224), channel_id=1, source_target_pairs={{0,4},{4,0},{1,5},{5,1},{2,6},{6,2},{3,7},{7,3}} | collective-permute-start | bytes 1572872 | tf_op jit(solution)/shard_map/ppermute | solution.py:243
  534.5 573.9 %collective-permute-start.22 = (bf16[896,2560]{1,0:T(8,128)(2,1)}, bf16[896,2560]{1,0:T(8,128)(2,1)}, u32[]{:S(2)}, u32[]{:S(2)}) collective-permute-start(bf16[896,2560]{1,0:T(8,128)(2,1)} %fusion.156), channel_id=1, source_target_pairs={{0,4},{4,0},{1,5},{5,1},{2,6},{6,2},{3,7},{7,3}} | collective-permute-start | bytes 13762568 | tf_op jit(solution)/shard_map/ppermute | solution.py:243
  544.5 565.7 %collective-permute-start.23 = (bf16[896,2560]{1,0:T(8,128)(2,1)}, bf16[896,2560]{1,0:T(8,128)(2,1)}, u32[]{:S(2)}, u32[]{:S(2)}) collective-permute-start(bf16[896,2560]{1,0:T(8,128)(2,1)} %fusion.159), channel_id=1, source_target_pairs={{0,4},{4,0},{1,5},{5,1},{2,6},{6,2},{3,7},{7,3}} | collective-permute-start | bytes 13762568 | tf_op jit(solution)/shard_map/ppermute | solution.py:243
  554.2 1059.5 %collective-permute-start.20 = (bf16[896,4352]{1,0:T(8,128)(2,1)}, bf16[896,4352]{1,0:T(8,128)(2,1)}, u32[]{:S(2)}, u32[]{:S(2)}) collective-permute-start(bf16[896,4352]{1,0:T(8,128)(2,1)} %fusion.112), channel_id=1, source_target_pairs={{0,4},{4,0},{1,5},{5,1},{2,6},{6,2},{3,7},{7,3}} | collective-permute-start | bytes 23396360 | tf_op jit(solution)/shard_map/ppermute | solution.py:243
  560.5 442.0 %collective-permute-start.16 = (bf16[896,1024]{1,0:T(8,128)(2,1)S(1)}, bf16[896,1024]{1,0:T(8,128)(2,1)S(1)}, u32[]{:S(2)}, u32[]{:S(2)}) collective-permute-start(bf16[896,1024]{1,0:T(8,128)(2,1)S(1)} %copy-done.7), channel_id=1, source_target_pairs={{0,4},{4,0},{1,5},{5,1},{2,6},{6,2},{3,7},{7,3}} | collective-permute-start | bytes 5505032 | tf_op jit(solution)/shard_map/ppermute | solution.py:243
  578.2 364.6 %collective-permute-start.45 = (bf16[128,1024]{1,0:T(8,128)(2,1)S(1)}, bf16[128,1024]{1,0:T(8,128)(2,1)S(1)}, u32[]{:S(2)}, u32[]{:S(2)}) collective-permute-start(bf16[128,1024]{1,0:T(8,128)(2,1)S(1)} %get-tuple-element.51), channel_id=1, source_target_pairs={{0,4},{4,0},{1,5},{5,1},{2,6},{6,2},{3,7},{7,3}} | collective-permute-start | bytes 786440 | tf_op jit(solution)/shard_map/ppermute | solution.py:243
  1087.1 546.0 %collective-permute-start.21 = (bf16[896,4352]{1,0:T(8,128)(2,1)}, bf16[896,4352]{1,0:T(8,128)(2,1)}, u32[]{:S(2)}, u32[]{:S(2)}) collective-permute-start(bf16[896,4352]{1,0:T(8,128)(2,1)} %fusion.115), channel_id=1, source_target_pairs={{0,4},{4,0},{1,5},{5,1},{2,6},{6,2},{3,7},{7,3}} | collective-permute-start | bytes 23396360 | tf_op jit(solution)/shard_map/ppermute | solution.py:243
  1096.7 328.5 %collective-permute-start.18 = (bf16[896,4352]{1,0:T(8,128)(2,1)}, bf16[896,4352]{1,0:T(8,128)(2,1)}, u32[]{:S(2)}, u32[]{:S(2)}) collective-permute-start(bf16[896,4352]{1,0:T(8,128)(2,1)} %fusion.106), channel_id=1, source_target_pairs={{0,4},{4,0},{1,5},{5,1},{2,6},{6,2},{3,7},{7,3}} | collective-permute-start | bytes 23396360 | tf_op jit(solution)/shard_map/ppermute | solution.py:243
  1108.4 483.9 %collective-permute-start.19 = (bf16[896,4352]{1,0:T(8,128)(2,1)}, bf16[896,4352]{1,0:T(8,128)(2,1)}, u32[]{:S(2)}, u32[]{:S(2)}) collective-permute-start(bf16[896,4352]{1,0:T(8,128)(2,1)} %fusion.109), channel_id=1, source_target_pairs={{0,4},{4,0},{1,5},{5,1},{2,6},{6,2},{3,7},{7,3}} | collective-permute-start | bytes 23396360 | tf_op jit(solution)/shard_map/ppermute | solution.py:243
  1134.5 750.3 %collective-permute-start.27 = (bf16[640,2560]{1,0:T(8,128)(2,1)}, bf16[640,2560]{1,0:T(8,128)(2,1)}, u32[]{:S(2)}, u32[]{:S(2)}) collective-permute-start(bf16[640,2560]{1,0:T(8,128)(2,1)} %multiply_convert_fusion.2), channel_id=1, source_target_pairs={{0,4},{4,0},{1,5},{5,1},{2,6},{6,2},{3,7},{7,3}} | collective-permute-start | bytes 9830408 | tf_op jit(solution)/shard_map/ppermute | solution.py:243
  1425.2 896.8 %collective-permute-start.34 = (bf16[256,2560]{1,0:T(8,128)(2,1)}, bf16[256,2560]{1,0:T(8,128)(2,1)}, u32[]{:S(2)}, u32[]{:S(2)}) collective-permute-start(bf16[256,2560]{1,0:T(8,128)(2,1)} %multiply_convert_fusion.5), channel_id=1, source_target_pairs={{0,4},{4,0},{1,5},{5,1},{2,6},{6,2},{3,7},{7,3}} | collective-permute-start | bytes 3932168 | tf_op jit(solution)/shard_map/ppermute | solution.py:243
  1612.0 373.8 %collective-permute-start.36 = (bf16[256,4352]{1,0:T(8,128)(2,1)}, bf16[256,4352]{1,0:T(8,128)(2,1)}, u32[]{:S(2)}, u32[]{:S(2)}) collective-permute-start(bf16[256,4352]{1,0:T(8,128)(2,1)} %multiply_convert_fusion.4), channel_id=1, source_target_pairs={{0,4},{4,0},{1,5},{5,1},{2,6},{6,2},{3,7},{7,3}} | collective-permute-start | bytes 6684680 | tf_op jit(solution)/shard_map/ppermute | solution.py:243
  1930.5 308.2 %collective-permute-start.29 = (bf16[640,4352]{1,0:T(8,128)(2,1)}, bf16[640,4352]{1,0:T(8,128)(2,1)}, u32[]{:S(2)}, u32[]{:S(2)}) collective-permute-start(bf16[640,4352]{1,0:T(8,128)(2,1)} %multiply_convert_fusion.1), channel_id=1, source_target_pairs={{0,4},{4,0},{1,5},{5,1},{2,6},{6,2},{3,7},{7,3}} | collective-permute-start | bytes 16711688 | tf_op jit(solution)/shard_map/ppermute | solution.py:243
  1975.5 293.7 %collective-permute-start.30 = (bf16[640,4352]{1,0:T(8,128)(2,1)}, bf16[640,4352]{1,0:T(8,128)(2,1)}, u32[]{:S(2)}, u32[]{:S(2)}) collective-permute-start(bf16[640,4352]{1,0:T(8,128)(2,1)} %multiply_convert_fusion), channel_id=1, source_target_pairs={{0,4},{4,0},{1,5},{5,1},{2,6},{6,2},{3,7},{7,3}} | collective-permute-start | bytes 16711688 | tf_op jit(solution)/shard_map/ppermute | solution.py:243
  1977.8 243.1 %collective-permute-start.37 = (bf16[256,4352]{1,0:T(8,128)(2,1)}, bf16[256,4352]{1,0:T(8,128)(2,1)}, u32[]{:S(2)}, u32[]{:S(2)}) collective-permute-start(bf16[256,4352]{1,0:T(8,128)(2,1)} %multiply_convert_fusion.3), channel_id=1, source_target_pairs={{0,4},{4,0},{1,5},{5,1},{2,6},{6,2},{3,7},{7,3}} | collective-permute-start | bytes 6684680 | tf_op jit(solution)/shard_map/ppermute | solution.py:243
  (40 other events, 1616.9 us)

commit v2 on v1

--- a/solution.py
+++ b/solution.py
@@ -9,8 +9,8 @@
 
 
 HEAD = 128
-HEAD_CUTS = (1024, 2048, 3072, 3072, 3072)
-HEAD_GO = (3072, 3072, 2048, 2048, 1024, 1024)
+HEAD_CUTS = (1024, 2048, 2048, 3072, 4096)
+HEAD_GO = (3072, 3072, 2048, 1792, 1280, 1024)
 BODY = (640, 256)
 BODY_CUTS = (1024, 4352, 4352, 2560)
 NB = 4
@@ -164,7 +164,7 @@
     me, mate, far = places()
     cols = o_ref.shape[1]
     depth = hb.shape[1]
-    order = ((mate + 2) % NB, mate, far, me)
+    order = ((mate + 2) % NB, far, mate, me)
     here = pltpu.make_async_copy(h_ref, hb, hsem)
     here.start()
     weights = []
@@ -183,14 +183,15 @@
             dst[:, at] = y.astype(dst.dtype)
 
     first = [remote(out.at[k], got.at[k], send, recv, k, mate) for k in range(2)]
-    for k in range(2):
-        term(k, out.at[k])
-        first[k].start()
-    term(2, mid)
+    term(0, out.at[0])
+    first[0].start()
+    term(1, mid)
     first[0].wait_recv()
     out[2] = (mid[...] + got[0].astype(F32)).astype(BF16)
     last = remote(out.at[2], got.at[2], send, recv, 2, far)
     last.start()
+    term(2, out.at[1])
+    first[1].start()
     term(3, mid)
     first[1].wait_recv()
     last.wait_recv()
@@ -281,31 +282,34 @@
     head_parts += [parts(xh, s) for i, s in enumerate(head_spans) if i]
     x_other = gather(body_rows)
     x_own = gather(own_rows)
-    body_parts = [parts(x_other, s) for s in body_spans]
+    body_parts = [parts(x_other, s) for s in body_spans[:-1]]
+    g, u = (
+        part(x_other, w, body_spans[-1])
+        for w in (wg, wu)
+    )
+    u, head_parts = fence((u, head_parts))
+    body_parts.append(swaps(g, u))
 
     def hidden(xs, s, rg, ru):
         g = f32dot(xs, col(wg, s))
         u = f32dot(xs, col(wu, s)) + ru.astype(F32)
         return (jax.nn.silu(g + rg.astype(F32)) * u).astype(BF16)
 
-    head_hid = [hidden(x_own[:HEAD], s, *head_parts[i]) for i, s in enumerate(head_spans)]
-    head_hid = jnp.concatenate(lax.optimization_barrier(head_hid), 1)
+    received = fence([jnp.concatenate(v, 1) for v in zip(*head_parts)])
+    head_hid = fence(hidden(x_own[:HEAD], (0, wg.shape[1]), *received))
     go_spans = spans(HEAD_GO)
     head_got = [swap(col(head_hid, s)) for s in go_spans]
 
     offs = spans(BODY)
-    body_hid = [[] for _ in BODY]
+    body_hid = []
     body_got = [[] for _ in BODY]
     for i, s in enumerate(body_spans):
+        body_hid.append(fence(hidden(x_own[HEAD:], s, *body_parts[i])))
         for j, o in enumerate(offs):
-            xs = x_own[HEAD + o[0] : HEAD + o[1]]
-            rg, ru = (row(v, o) for v in body_parts[i])
-            h = hidden(xs, s, rg, ru)
-            body_hid[j].append(h)
-            body_got[j].append(swap(h))
+            body_got[j].append(swap(row(body_hid[i], o)))
 
     out = jnp.zeros((x.shape[0], cols), BF16)
-    h = jnp.concatenate([head_hid] + [jnp.concatenate(v, 1) for v in body_hid])
+    h = jnp.concatenate([head_hid, jnp.concatenate(body_hid, 1)])
     r = scatter(f32dot(h, wd))
     out = lax.dynamic_update_slice(out, r[:HEAD], (HEAD * a, 0))
     out = lax.dynamic_update_slice(out, r[HEAD:], (base + half * a, 0))

time: 2420 us -> 2200 us (0.909)
  waiting for transfers between devices: 1210 us -> 1080 us
  matrix products: 1060 us -> 959 us
    ppermute x32, waiting for transfers between devices: 1090 us -> 955 us  [body(): swap = lambda v: lax.ppermute(v, 'a', [(0, 1), (1, 0)])]
    dot_general x56 -> x40, matrix products: 1060 us -> 959 us  [f32dot(): return jnp.dot(l, r, preferred_element_type=F32)]
  transfers between devices with their start and end apart: 47 -> 47, of which waited for: 19 -> 21; matrix products, arithmetic and copies ran while one was open for 47% -> 48% of each run, Pallas kernels for 0% -> 0%
where the time goes in v2:
time: 2200 us; the launch traced here: 2190 us
  waiting for transfers between devices  1080 us (49%)
  matrix products  959 us (44%)
  local copies, waits for them, and re-layouts  68 us (3%)
  starting transfers between devices  36.9 us (2%)
  other arithmetic  28.1 us (1%)
  Pallas kernels  24.3 us (1%)
    dot_general x40, matrix products, f32dot(): return jnp.dot(l, r, preferred_element_type=F32)  959 us
    ppermute x32, waiting for transfers between devices, body(): swap = lambda v: lax.ppermute(v, 'a', [(0, 1), (1, 0)])  955 us
    ppermute x15, waiting for transfers between devices, shift(): return lax.ppermute(v, 'b', [(i, (i + k) % NB) for i in range(NB)])  121 us
  transfers between devices with their start and end apart: 47, of which 21 were waited for; matrix products, arithmetic and copies ran while one was open for 48% of the time, Pallas kernels for 0%

profile of v2, /device:TPU:0, one launch (start us, length us, event | category | flops | bytes accessed | tf_op | source)
XLA Modules:
  0.0 2192.2 jit_solution(4371589085450233728)
XLA Ops:
  143.7 39.3 %fusion.85 = bf16[896,4352]{1,0:T(8,128)(2,1)} fusion(bf16[896,4096]{1,0:T(8,128)(2,1)S(1)} %constant_dynamic-update-slice_fusion.11, bf16[4096,12288]{1,0:T(8,128)(2,1)} %wu_ref.1), kind=kOutput, calls=%fused_computation.81 | convolution fusion | flops 31947718656 | bytes 50790400 | tf_op jit(solution)/shard_map/dot_general | solution.py:229
  183.0 39.0 %fusion.82 = bf16[896,4352]{1,0:T(8,128)(2,1)} fusion(bf16[896,4096]{1,0:T(8,128)(2,1)S(1)} %constant_dynamic-update-slice_fusion.11, bf16[4096,12288]{1,0:T(8,128)(2,1)} %wg_ref.1), kind=kOutput, calls=%fused_computation.80 | convolution fusion | flops 31947718656 | bytes 50790400 | tf_op jit(solution)/shard_map/dot_general | solution.py:229
  222.0 39.2 %fusion.79 = bf16[896,4352]{1,0:T(8,128)(2,1)} fusion(bf16[896,4096]{1,0:T(8,128)(2,1)S(1)} %constant_dynamic-update-slice_fusion.11, bf16[4096,12288]{1,0:T(8,128)(2,1)} %wu_ref.1), kind=kOutput, calls=%fused_computation.79 | convolution fusion | flops 31947718656 | bytes 50790400 | tf_op jit(solution)/shard_map/dot_general | solution.py:229
  261.2 39.1 %fusion.76 = bf16[896,4352]{1,0:T(8,128)(2,1)} fusion(bf16[896,4096]{1,0:T(8,128)(2,1)S(1)} %constant_dynamic-update-slice_fusion.11, bf16[4096,12288]{1,0:T(8,128)(2,1)} %wg_ref.1), kind=kOutput, calls=%fused_computation.78 | convolution fusion | flops 31947718656 | bytes 50790400 | tf_op jit(solution)/shard_map/dot_general | solution.py:229
  300.3 23.1 %fusion.105 = bf16[896,2560]{1,0:T(8,128)(2,1)} fusion(bf16[896,4096]{1,0:T(8,128)(2,1)S(1)} %constant_dynamic-update-slice_fusion.11, bf16[4096,12288]{1,0:T(8,128)(2,1)} %wg_ref.1), kind=kOutput, calls=%fused_computation.96 | convolution fusion | flops 18792775680 | bytes 32899072 | tf_op jit(solution)/shard_map/dot_general | solution.py:229
  447.9 25.5 %fusion.52 = f32[896,2560]{1,0:T(8,128)} fusion(bf16[4096,12288]{1,0:T(8,128)(2,1)} %wg_ref.1, bf16[1024,4096]{1,0:T(8,128)(2,1)} %constant_dynamic-update-slice_fusion.15), kind=kOutput, calls=%fused_computation.52 | convolution fusion | flops 18790481920 | bytes 37486592 | tf_op jit(solution)/shard_map/dot_general | solution.py:229
  473.4 41.5 %fusion.18 = f32[896,4352]{1,0:T(8,128)} fusion(bf16[4096,12288]{1,0:T(8,128)(2,1)} %wg_ref.1, bf16[1024,4096]{1,0:T(8,128)(2,1)} %constant_dynamic-update-slice_fusion.15), kind=kOutput, calls=%fused_computation.18 | convolution fusion | flops 31943819264 | bytes 58589184 | tf_op jit(solution)/shard_map/dot_general | solution.py:229
  514.9 41.3 %fusion.26 = f32[896,4352]{1,0:T(8,128)} fusion(bf16[4096,12288]{1,0:T(8,128)(2,1)} %wg_ref.1, bf16[1024,4096]{1,0:T(8,128)(2,1)} %constant_dynamic-update-slice_fusion.15), kind=kOutput, calls=%fused_computation.26 | convolution fusion | flops 31943819264 | bytes 58589184 | tf_op jit(solution)/shard_map/dot_general | solution.py:229
  569.7 36.9 %convolution_add_fusion.1 = f32[128,12288]{1,0:T(8,128)} fusion(bf16[4096,12288]{1,0:T(8,128)(2,1)} %wg_ref.1, bf16[128,12288]{1,0:T(8,128)(2,1)} %get-tuple-element.46, bf16[1024,4096]{1,0:T(8,128)(2,1)} %constant_dynamic-update-slice_fusion.15), kind=kOutput, calls=%fused_computation.73 | convolution fusion | flops 12888047616 | bytes 111149056 | tf_op jit(solution)/shard_map/dot_general | solution.py:229
  606.6 36.0 %multiply_convert_fusion.3 = bf16[128,12288]{1,0:T(8,128)(2,1)S(1)} fusion(f32[128,12288]{1,0:T(8,128)} %convolution_add_fusion.1, bf16[128,12288]{1,0:T(8,128)(2,1)} %get-tuple-element.47, bf16[4096,12288]{1,0:T(8,128)(2,1)} %wu_ref.1, bf16[1024,4096]{1,0:T(8,128)(2,1)} %constant_dynamic-update-slice_fusion.15), kind=kOutput, calls=%fused_computation.94 | convolution fusion | flops 12897484800 | bytes 114294784 | tf_op jit(solution)/shard_map/dot_general | solution.py:229
  644.4 53.4 %collective-permute-done.45 = bf16[128,1280]{1,0:T(8,128)(2,1)S(1)} collective-permute-done((bf16[128,1280]{1,0:T(8,128)(2,1)S(1)}, bf16[128,1280]{1,0:T(8,128)(2,1)S(1)}, u32[]{:S(2)}, u32[]{:S(2)}) %collective-permute-start.45) | collective-permute-done | bytes 327712 | tf_op jit(solution)/shard_map/ppermute | solution.py:244
  744.8 163.3 %collective-permute-done.41 = bf16[128,3072]{1,0:T(8,128)(2,1)S(1)} collective-permute-done((bf16[128,3072]{1,0:T(8,128)(2,1)S(1)}, bf16[128,3072]{1,0:T(8,128)(2,1)S(1)}, u32[]{:S(2)}, u32[]{:S(2)}) %collective-permute-start.41) | collective-permute-done | bytes 786464 | tf_op jit(solution)/shard_map/ppermute | solution.py:244
  956.1 172.4 %collective-permute-done.28 = bf16[640,1024]{1,0:T(8,128)(2,1)S(1)} collective-permute-done((bf16[640,1024]{1,0:T(8,128)(2,1)S(1)}, bf16[640,1024]{1,0:T(8,128)(2,1)S(1)}, u32[]{:S(2)}, u32[]{:S(2)}) %collective-permute-start.28) | collective-permute-done | bytes 1310752 | tf_op jit(solution)/shard_map/ppermute | solution.py:244
  1142.2 27.3 %multiply_convert_fusion.2 = bf16[896,2560]{1,0:T(8,128)(2,1)S(1)} fusion(bf16[896,2560]{1,0:T(8,128)(2,1)} %collective-permute-done.23, f32[896,2560]{1,0:T(8,128)} %fusion.52, bf16[896,2560]{1,0:T(8,128)(2,1)} %collective-permute-done.22, bf16[4096,12288]{1,0:T(8,128)(2,1)} %wu_ref.1, bf16[1024,4096]{1,0:T(8,128)(2,1)} %constant_dynamic-update-slice_fusion.15), kind=kOutput, calls=%fused_computation.77 | convolution fusion | flops 18813419520 | bytes 51249152 | tf_op jit(solution)/shard_map/dot_general | solution.py:229
  1175.8 45.0 %multiply_convert_fusion = bf16[896,4352]{1,0:T(8,128)(2,1)} fusion(bf16[896,4352]{1,0:T(8,128)(2,1)} %collective-permute-done.21, f32[896,4352]{1,0:T(8,128)} %fusion.18, bf16[896,4352]{1,0:T(8,128)(2,1)} %collective-permute-done.20, bf16[4096,12288]{1,0:T(8,128)(2,1)} %wu_ref.1, bf16[1024,4096]{1,0:T(8,128)(2,1)} %constant_dynamic-update-slice_fusion.15), kind=kOutput, calls=%fused_computation.68 | convolution fusion | flops 31982813184 | bytes 81985536 | tf_op jit(solution)/shard_map/dot_general | solution.py:229
  1220.7 78.8 %collective-permute-done.19 = bf16[896,4352]{1,0:T(8,128)(2,1)} collective-permute-done((bf16[896,4352]{1,0:T(8,128)(2,1)}, bf16[896,4352]{1,0:T(8,128)(2,1)}, u32[]{:S(2)}, u32[]{:S(2)}) %collective-permute-start.19) | collective-permute-done | bytes 7798816 | tf_op jit(solution)/shard_map/ppermute | solution.py:244
  1299.5 167.1 %collective-permute-done.18 = bf16[896,4352]{1,0:T(8,128)(2,1)} collective-permute-done((bf16[896,4352]{1,0:T(8,128)(2,1)}, bf16[896,4352]{1,0:T(8,128)(2,1)}, u32[]{:S(2)}, u32[]{:S(2)}) %collective-permute-start.18) | collective-permute-done | bytes 7798816 | tf_op jit(solution)/shard_map/ppermute | solution.py:244
  1466.6 45.2 %multiply_convert_fusion.1 = bf16[896,4352]{1,0:T(8,128)(2,1)} fusion(bf16[896,4352]{1,0:T(8,128)(2,1)} %collective-permute-done.19, f32[896,4352]{1,0:T(8,128)} %fusion.26, bf16[896,4352]{1,0:T(8,128)(2,1)} %collective-permute-done.18, bf16[4096,12288]{1,0:T(8,128)(2,1)} %wu_ref.1, bf16[1024,4096]{1,0:T(8,128)(2,1)} %constant_dynamic-update-slice_fusion.15), kind=kOutput, calls=%fused_computation.69 | convolution fusion | flops 31982813184 | bytes 81985536 | tf_op jit(solution)/shard_map/dot_general | solution.py:229
  1511.9 128.1 %fusion.28 = f32[1024,4096]{1,0:T(8,128)} fusion(bf16[12288,4096]{1,0:T(8,128)(2,1)} %w_ref.1, bf16[896,2560]{1,0:T(8,128)(2,1)} %copy-done.5, bf16[896,4352]{1,0:T(8,128)(2,1)} %multiply_convert_fusion, bf16[896,4352]{1,0:T(8,128)(2,1)} %multiply_convert_fusion.1, bf16[896,1024]{1,0:T(8,128)(2,1)} %copy-done.11, bf16[128,12288]{1,0:T(8,128)(2,1)S(1)} %copy-done.8), kind=kOutput, calls=%fused_computation.28 | convolution fusion | flops 103205044224 | bytes 142606336 | tf_op jit(solution)/shard_map/dot_general | solution.py:229
  1704.0 45.4 %collective-permute-done.25 = bf16[1024,1024]{1,0:T(8,128)(2,1)} collective-permute-done((bf16[1024,1024]{1,0:T(8,128)(2,1)}, bf16[1024,1024]{1,0:T(8,128)(2,1)}, u32[]{:S(2)}, u32[]{:S(2)}) %collective-permute-start.25) | collective-permute-done | bytes 2097184 | tf_op jit(solution)/shard_map/ppermute | solution.py:251
  1777.8 218.6 %collective-permute-done.37 = bf16[256,4352]{1,0:T(8,128)(2,1)} collective-permute-done((bf16[256,4352]{1,0:T(8,128)(2,1)}, bf16[256,4352]{1,0:T(8,128)(2,1)}, u32[]{:S(2)}, u32[]{:S(2)}) %collective-permute-start.37) | collective-permute-done | bytes 2228256 | tf_op jit(solution)/shard_map/ppermute | solution.py:244
  2014.5 30.3 %fusion.10 = f32[640,4096]{1,0:T(8,128)} fusion(bf16[640,4352]{1,0:T(8,128)(2,1)} %collective-permute-done.29, bf16[12288,4096]{1,0:T(8,128)(2,1)} %w_ref.1), kind=kOutput, calls=%fused_computation.10 | convolution fusion | flops 22817013760 | bytes 51707904 | tf_op jit(solution)/shard_map/dot_general | solution.py:229
  2044.8 30.3 %fusion.6 = f32[640,4096]{1,0:T(8,128)} fusion(bf16[640,4352]{1,0:T(8,128)(2,1)} %collective-permute-done.30, bf16[12288,4096]{1,0:T(8,128)(2,1)} %w_ref.1), kind=kOutput, calls=%fused_computation.6 | convolution fusion | flops 22817013760 | bytes 51707904 | tf_op jit(solution)/shard_map/dot_general | solution.py:229
  2129.3 26.6 %collective-permute-done.32 = bf16[640,1024]{1,0:T(8,128)(2,1)} collective-permute-done((bf16[640,1024]{1,0:T(8,128)(2,1)}, bf16[640,1024]{1,0:T(8,128)(2,1)}, u32[]{:S(2)}, u32[]{:S(2)}) %collective-permute-start.32) | collective-permute-done | bytes 1310752 | tf_op jit(solution)/shard_map/ppermute | solution.py:251
  (201 shorter events, 598.8 us)
Async XLA Ops:
  15.2 102.2 %collective-permute-start.5 = (bf16[896,1024]{1,0:T(8,128)(2,1)}, bf16[896,1024]{1,0:T(8,128)(2,1)}, u32[]{:S(2)}, u32[]{:S(2)}) collective-permute-start(bf16[896,1024]{1,0:T(8,128)(2,1)} %get-tuple-element.32), channel_id=1, source_target_pairs={{0,3},{1,0},{2,1},{3,2},{4,7},{5,4},{6,5},{7,6}} | collective-permute-start | bytes 5505032 | tf_op jit(solution)/shard_map/ppermute | solution.py:251
  15.8 307.6 %collective-permute-start.6 = (bf16[128,1024]{1,0:T(8,128)(2,1)}, bf16[128,1024]{1,0:T(8,128)(2,1)}, u32[]{:S(2)}, u32[]{:S(2)}) collective-permute-start(bf16[128,1024]{1,0:T(8,128)(2,1)} %get-tuple-element.33), channel_id=1, source_target_pairs={{0,4},{4,0},{1,5},{5,1},{2,6},{6,2},{3,7},{7,3}} | collective-permute-start | bytes 786440 | tf_op jit(solution)/shard_map/ppermute | solution.py:244
  17.4 306.6 %collective-permute-start.7 = (bf16[128,1024]{1,0:T(8,128)(2,1)}, bf16[128,1024]{1,0:T(8,128)(2,1)}, u32[]{:S(2)}, u32[]{:S(2)}) collective-permute-start(bf16[128,1024]{1,0:T(8,128)(2,1)} %get-tuple-element.34), channel_id=1, source_target_pairs={{0,4},{4,0},{1,5},{5,1},{2,6},{6,2},{3,7},{7,3}} | collective-permute-start | bytes 786440 | tf_op jit(solution)/shard_map/ppermute | solution.py:244
  111.9 213.6 %collective-permute-start.8 = (bf16[128,2048]{1,0:T(8,128)(2,1)}, bf16[128,2048]{1,0:T(8,128)(2,1)}, u32[]{:S(2)}, u32[]{:S(2)}) collective-permute-start(bf16[128,2048]{1,0:T(8,128)(2,1)} %fusion.129), channel_id=1, source_target_pairs={{0,4},{4,0},{1,5},{5,1},{2,6},{6,2},{3,7},{7,3}} | collective-permute-start | bytes 1572872 | tf_op jit(solution)/shard_map/ppermute | solution.py:244
  115.2 210.8 %collective-permute-start.9 = (bf16[128,2048]{1,0:T(8,128)(2,1)}, bf16[128,2048]{1,0:T(8,128)(2,1)}, u32[]{:S(2)}, u32[]{:S(2)}) collective-permute-start(bf16[128,2048]{1,0:T(8,128)(2,1)} %fusion.132), channel_id=1, source_target_pairs={{0,4},{4,0},{1,5},{5,1},{2,6},{6,2},{3,7},{7,3}} | collective-permute-start | bytes 1572872 | tf_op jit(solution)/shard_map/ppermute | solution.py:244
  117.4 210.1 %collective-permute-start.10 = (bf16[128,2048]{1,0:T(8,128)(2,1)}, bf16[128,2048]{1,0:T(8,128)(2,1)}, u32[]{:S(2)}, u32[]{:S(2)}) collective-permute-start(bf16[128,2048]{1,0:T(8,128)(2,1)} %fusion.135), channel_id=1, source_target_pairs={{0,4},{4,0},{1,5},{5,1},{2,6},{6,2},{3,7},{7,3}} | collective-permute-start | bytes 1572872 | tf_op jit(solution)/shard_map/ppermute | solution.py:244
  339.5 101.7 %collective-permute-start = (bf16[1024,1024]{1,0:T(8,128)(2,1)S(1)}, bf16[1024,1024]{1,0:T(8,128)(2,1)S(1)}, u32[]{:S(2)}, u32[]{:S(2)}) collective-permute-start(bf16[1024,1024]{1,0:T(8,128)(2,1)S(1)} %copy-done.10), channel_id=1, source_target_pairs={{0,1},{1,2},{2,3},{3,0},{4,5},{5,6},{6,7},{7,4}} | collective-permute-start | bytes 6291464 | tf_op jit(solution)/shard_map/ppermute | solution.py:251
  414.5 726.2 %collective-permute-start.23 = (bf16[896,2560]{1,0:T(8,128)(2,1)}, bf16[896,2560]{1,0:T(8,128)(2,1)}, u32[]{:S(2)}, u32[]{:S(2)}) collective-permute-start(bf16[896,2560]{1,0:T(8,128)(2,1)} %fusion.102), channel_id=1, source_target_pairs={{0,4},{4,0},{1,5},{5,1},{2,6},{6,2},{3,7},{7,3}} | collective-permute-start | bytes 13762568 | tf_op jit(solution)/shard_map/ppermute | solution.py:244
  415.0 727.2 %collective-permute-start.22 = (bf16[896,2560]{1,0:T(8,128)(2,1)}, bf16[896,2560]{1,0:T(8,128)(2,1)}, u32[]{:S(2)}, u32[]{:S(2)}) collective-permute-start(bf16[896,2560]{1,0:T(8,128)(2,1)} %fusion.105), channel_id=1, source_target_pairs={{0,4},{4,0},{1,5},{5,1},{2,6},{6,2},{3,7},{7,3}} | collective-permute-start | bytes 13762568 | tf_op jit(solution)/shard_map/ppermute | solution.py:244
  441.1 286.8 %collective-permute-start.17 = (bf16[896,1024]{1,0:T(8,128)(2,1)}, bf16[896,1024]{1,0:T(8,128)(2,1)}, u32[]{:S(2)}, u32[]{:S(2)}) collective-permute-start(bf16[896,1024]{1,0:T(8,128)(2,1)} %fusion.146), channel_id=1, source_target_pairs={{0,4},{4,0},{1,5},{5,1},{2,6},{6,2},{3,7},{7,3}} | collective-permute-start | bytes 5505032 | tf_op jit(solution)/shard_map/ppermute | solution.py:244
  443.2 286.3 %collective-permute-start.16 = (bf16[896,1024]{1,0:T(8,128)(2,1)}, bf16[896,1024]{1,0:T(8,128)(2,1)}, u32[]{:S(2)}, u32[]{:S(2)}) collective-permute-start(bf16[896,1024]{1,0:T(8,128)(2,1)} %fusion.143), channel_id=1, source_target_pairs={{0,4},{4,0},{1,5},{5,1},{2,6},{6,2},{3,7},{7,3}} | collective-permute-start | bytes 5505032 | tf_op jit(solution)/shard_map/ppermute | solution.py:244
  720.4 453.9 %collective-permute-start.21 = (bf16[896,4352]{1,0:T(8,128)(2,1)}, bf16[896,4352]{1,0:T(8,128)(2,1)}, u32[]{:S(2)}, u32[]{:S(2)}) collective-permute-start(bf16[896,4352]{1,0:T(8,128)(2,1)} %fusion.85), channel_id=1, source_target_pairs={{0,4},{4,0},{1,5},{5,1},{2,6},{6,2},{3,7},{7,3}} | collective-permute-start | bytes 23396360 | tf_op jit(solution)/shard_map/ppermute | solution.py:244
  728.0 180.2 %collective-permute-start.41 = (bf16[128,3072]{1,0:T(8,128)(2,1)S(1)}, bf16[128,3072]{1,0:T(8,128)(2,1)S(1)}, u32[]{:S(2)}, u32[]{:S(2)}) collective-permute-start(bf16[128,3072]{1,0:T(8,128)(2,1)S(1)} %get-tuple-element.67), channel_id=1, source_target_pairs={{0,4},{4,0},{1,5},{5,1},{2,6},{6,2},{3,7},{7,3}} | collective-permute-start | bytes 2359304 | tf_op jit(solution)/shard_map/ppermute | solution.py:244
  729.5 195.5 %collective-permute-start.42 = (bf16[128,3072]{1,0:T(8,128)(2,1)S(1)}, bf16[128,3072]{1,0:T(8,128)(2,1)S(1)}, u32[]{:S(2)}, u32[]{:S(2)}) collective-permute-start(bf16[128,3072]{1,0:T(8,128)(2,1)S(1)} %get-tuple-element.66), channel_id=1, source_target_pairs={{0,4},{4,0},{1,5},{5,1},{2,6},{6,2},{3,7},{7,3}} | collective-permute-start | bytes 2359304 | tf_op jit(solution)/shard_map/ppermute | solution.py:244
  925.0 250.8 %collective-permute-start.20 = (bf16[896,4352]{1,0:T(8,128)(2,1)}, bf16[896,4352]{1,0:T(8,128)(2,1)}, u32[]{:S(2)}, u32[]{:S(2)}) collective-permute-start(bf16[896,4352]{1,0:T(8,128)(2,1)} %fusion.82), channel_id=1, source_target_pairs={{0,4},{4,0},{1,5},{5,1},{2,6},{6,2},{3,7},{7,3}} | collective-permute-start | bytes 23396360 | tf_op jit(solution)/shard_map/ppermute | solution.py:244
  936.2 192.3 %collective-permute-start.28 = (bf16[640,1024]{1,0:T(8,128)(2,1)S(1)}, bf16[640,1024]{1,0:T(8,128)(2,1)S(1)}, u32[]{:S(2)}, u32[]{:S(2)}) collective-permute-start(bf16[640,1024]{1,0:T(8,128)(2,1)S(1)} %slice.192), channel_id=1, source_target_pairs={{0,4},{4,0},{1,5},{5,1},{2,6},{6,2},{3,7},{7,3}} | collective-permute-start | bytes 3932168 | tf_op jit(solution)/shard_map/ppermute | solution.py:244
  1128.5 171.0 %collective-permute-start.19 = (bf16[896,4352]{1,0:T(8,128)(2,1)}, bf16[896,4352]{1,0:T(8,128)(2,1)}, u32[]{:S(2)}, u32[]{:S(2)}) collective-permute-start(bf16[896,4352]{1,0:T(8,128)(2,1)} %fusion.79), channel_id=1, source_target_pairs={{0,4},{4,0},{1,5},{5,1},{2,6},{6,2},{3,7},{7,3}} | collective-permute-start | bytes 23396360 | tf_op jit(solution)/shard_map/ppermute | solution.py:244
  1140.6 326.0 %collective-permute-start.18 = (bf16[896,4352]{1,0:T(8,128)(2,1)}, bf16[896,4352]{1,0:T(8,128)(2,1)}, u32[]{:S(2)}, u32[]{:S(2)}) collective-permute-start(bf16[896,4352]{1,0:T(8,128)(2,1)} %fusion.76), channel_id=1, source_target_pairs={{0,4},{4,0},{1,5},{5,1},{2,6},{6,2},{3,7},{7,3}} | collective-permute-start | bytes 23396360 | tf_op jit(solution)/shard_map/ppermute | solution.py:244
  1173.7 484.8 %collective-permute-start.27 = (bf16[640,2560]{1,0:T(8,128)(2,1)}, bf16[640,2560]{1,0:T(8,128)(2,1)}, u32[]{:S(2)}, u32[]{:S(2)}) collective-permute-start(bf16[640,2560]{1,0:T(8,128)(2,1)} %slice.191), channel_id=1, source_target_pairs={{0,4},{4,0},{1,5},{5,1},{2,6},{6,2},{3,7},{7,3}} | collective-permute-start | bytes 9830408 | tf_op jit(solution)/shard_map/ppermute | solution.py:244
  1174.2 923.6 %collective-permute-start.34 = (bf16[256,2560]{1,0:T(8,128)(2,1)}, bf16[256,2560]{1,0:T(8,128)(2,1)}, u32[]{:S(2)}, u32[]{:S(2)}) collective-permute-start(bf16[256,2560]{1,0:T(8,128)(2,1)} %slice.195), channel_id=1, source_target_pairs={{0,4},{4,0},{1,5},{5,1},{2,6},{6,2},{3,7},{7,3}} | collective-permute-start | bytes 3932168 | tf_op jit(solution)/shard_map/ppermute | solution.py:244
  1658.5 101.4 %collective-permute-start.36 = (bf16[256,4352]{1,0:T(8,128)(2,1)S(1)}, bf16[256,4352]{1,0:T(8,128)(2,1)}, u32[]{:S(2)}, u32[]{:S(2)}) collective-permute-start(bf16[256,4352]{1,0:T(8,128)(2,1)S(1)} %slice.197), channel_id=1, source_target_pairs={{0,4},{4,0},{1,5},{5,1},{2,6},{6,2},{3,7},{7,3}} | collective-permute-start | bytes 6684680 | tf_op jit(solution)/shard_map/ppermute | solution.py:244
  1703.3 311.2 %collective-permute-start.29 = (bf16[640,4352]{1,0:T(8,128)(2,1)}, bf16[640,4352]{1,0:T(8,128)(2,1)}, u32[]{:S(2)}, u32[]{:S(2)}) collective-permute-start(bf16[640,4352]{1,0:T(8,128)(2,1)} %slice.193), channel_id=1, source_target_pairs={{0,4},{4,0},{1,5},{5,1},{2,6},{6,2},{3,7},{7,3}} | collective-permute-start | bytes 16711688 | tf_op jit(solution)/shard_map/ppermute | solution.py:244
  1749.3 295.5 %collective-permute-start.30 = (bf16[640,4352]{1,0:T(8,128)(2,1)}, bf16[640,4352]{1,0:T(8,128)(2,1)}, u32[]{:S(2)}, u32[]{:S(2)}) collective-permute-start(bf16[640,4352]{1,0:T(8,128)(2,1)} %slice.194), channel_id=1, source_target_pairs={{0,4},{4,0},{1,5},{5,1},{2,6},{6,2},{3,7},{7,3}} | collective-permute-start | bytes 16711688 | tf_op jit(solution)/shard_map/ppermute | solution.py:244
  1750.0 246.4 %collective-permute-start.37 = (bf16[256,4352]{1,0:T(8,128)(2,1)}, bf16[256,4352]{1,0:T(8,128)(2,1)}, u32[]{:S(2)}, u32[]{:S(2)}) collective-permute-start(bf16[256,4352]{1,0:T(8,128)(2,1)} %slice.198), channel_id=1, source_target_pairs={{0,4},{4,0},{1,5},{5,1},{2,6},{6,2},{3,7},{7,3}} | collective-permute-start | bytes 6684680 | tf_op jit(solution)/shard_map/ppermute | solution.py:244
  (44 other events, 2147.4 us)

commit v3 on v1

--- a/solution.py
+++ b/solution.py
@@ -9,8 +9,8 @@
 
 
 HEAD = 128
-HEAD_CUTS = (1024, 2048, 3072, 3072, 3072)
-HEAD_GO = (3072, 3072, 2048, 2048, 1024, 1024)
+HEAD_CUTS = (1024, 2048, 2048, 3072, 4096)
+HEAD_GO = (3072, 3072, 2048, 1792, 1280, 1024)
 BODY = (640, 256)
 BODY_CUTS = (1024, 4352, 4352, 2560)
 NB = 4
@@ -164,7 +164,7 @@
     me, mate, far = places()
     cols = o_ref.shape[1]
     depth = hb.shape[1]
-    order = ((mate + 2) % NB, mate, far, me)
+    order = ((mate + 2) % NB, far, mate, me)
     here = pltpu.make_async_copy(h_ref, hb, hsem)
     here.start()
     weights = []
@@ -183,14 +183,15 @@
             dst[:, at] = y.astype(dst.dtype)
 
     first = [remote(out.at[k], got.at[k], send, recv, k, mate) for k in range(2)]
-    for k in range(2):
-        term(k, out.at[k])
-        first[k].start()
-    term(2, mid)
+    term(0, out.at[0])
+    first[0].start()
+    term(1, mid)
     first[0].wait_recv()
     out[2] = (mid[...] + got[0].astype(F32)).astype(BF16)
     last = remote(out.at[2], got.at[2], send, recv, 2, far)
     last.start()
+    term(2, out.at[1])
+    first[1].start()
     term(3, mid)
     first[1].wait_recv()
     last.wait_recv()

time: 2420 us -> 2420 us (level)
  transfers between devices with their start and end apart: 47 -> 47, of which waited for: 19 -> 20; matrix products, arithmetic and copies ran while one was open for 47% -> 47% of each run, Pallas kernels for 0% -> 0%
where the time goes in v3:
time: 2420 us; the launch traced here: 2410 us
  waiting for transfers between devices  1210 us (50%)
  matrix products  1070 us (44%)
  local copies, waits for them, and re-layouts  46.1 us (2%)
  starting transfers between devices  41.6 us (2%)
  other arithmetic  27.5 us (1%)
    ppermute x32, waiting for transfers between devices, body(): swap = lambda v: lax.ppermute(v, 'a', [(0, 1), (1, 0)])  1090 us
    dot_general x56, matrix products, f32dot(): return jnp.dot(l, r, preferred_element_type=F32)  1070 us
    ppermute x15, waiting for transfers between devices, shift(): return lax.ppermute(v, 'b', [(i, (i + k) % NB) for i in range(NB)])  120 us
  transfers between devices with their start and end apart: 47, of which 20 were waited for; matrix products, arithmetic and copies ran while one was open for 47% of the time, Pallas kernels for 0%

profile of v3, /device:TPU:0, one launch (start us, length us, event | category | flops | bytes accessed | tf_op | source)
XLA Modules:
  0.0 2413.1 jit_solution(4189872639798306100)
XLA Ops:
  121.5 22.9 fusion.156
  144.4 23.0 fusion.159
  167.4 39.2 %fusion.114 = bf16[896,4352]{1,0:T(8,128)(2,1)} fusion(bf16[896,4096]{1,0:T(8,128)(2,1)S(1)} %constant_dynamic-update-slice_fusion.6, bf16[4096,12288]{1,0:T(8,128)(2,1)} %wg_ref.1), kind=kOutput, calls=%fused_computation.113 | convolution fusion | flops 31947718656 | bytes 50790400 | tf_op jit(solution)/shard_map/dot_general | solution.py:229
  206.6 39.0 %fusion.117 = bf16[896,4352]{1,0:T(8,128)(2,1)} fusion(bf16[896,4096]{1,0:T(8,128)(2,1)S(1)} %constant_dynamic-update-slice_fusion.6, bf16[4096,12288]{1,0:T(8,128)(2,1)} %wu_ref.1), kind=kOutput, calls=%fused_computation.114 | convolution fusion | flops 31947718656 | bytes 50790400 | tf_op jit(solution)/shard_map/dot_general | solution.py:229
  245.6 39.2 %fusion.108 = bf16[896,4352]{1,0:T(8,128)(2,1)} fusion(bf16[896,4096]{1,0:T(8,128)(2,1)S(1)} %constant_dynamic-update-slice_fusion.6, bf16[4096,12288]{1,0:T(8,128)(2,1)} %wg_ref.1), kind=kOutput, calls=%fused_computation.111 | convolution fusion | flops 31947718656 | bytes 50790400 | tf_op jit(solution)/shard_map/dot_general | solution.py:229
  284.8 39.0 %fusion.111 = bf16[896,4352]{1,0:T(8,128)(2,1)} fusion(bf16[896,4096]{1,0:T(8,128)(2,1)S(1)} %constant_dynamic-update-slice_fusion.6, bf16[4096,12288]{1,0:T(8,128)(2,1)} %wu_ref.1), kind=kOutput, calls=%fused_computation.112 | convolution fusion | flops 31947718656 | bytes 50790400 | tf_op jit(solution)/shard_map/dot_general | solution.py:229
  359.2 30.8 %fusion.26 = f32[640,4352]{1,0:T(8,128)} fusion(bf16[4096,12288]{1,0:T(8,128)(2,1)} %wg_ref.1, bf16[1024,4096]{1,0:T(8,128)(2,1)} %constant_dynamic-update-slice_fusion.10), kind=kOutput, calls=%fused_computation.26 | convolution fusion | flops 22817013760 | bytes 52035584 | tf_op jit(solution)/shard_map/dot_general | solution.py:229
  390.0 30.9 %fusion.38 = f32[640,4352]{1,0:T(8,128)} fusion(bf16[4096,12288]{1,0:T(8,128)(2,1)} %wg_ref.1, bf16[1024,4096]{1,0:T(8,128)(2,1)} %constant_dynamic-update-slice_fusion.10), kind=kOutput, calls=%fused_computation.38 | convolution fusion | flops 22817013760 | bytes 52035584 | tf_op jit(solution)/shard_map/dot_general | solution.py:229
  420.9 21.5 fusion.86
  573.5 375.4 %collective-permute-done.45 = bf16[128,1280]{1,0:T(8,128)(2,1)S(1)} collective-permute-done((bf16[128,1280]{1,0:T(8,128)(2,1)S(1)}, bf16[128,1280]{1,0:T(8,128)(2,1)S(1)}, u32[]{:S(2)}, u32[]{:S(2)}) %collective-permute-start.45) | collective-permute-done | bytes 327712 | tf_op jit(solution)/shard_map/ppermute | solution.py:244
  1001.9 30.7 %collective-permute-done.17 = bf16[896,1024]{1,0:T(8,128)(2,1)S(1)} collective-permute-done((bf16[896,1024]{1,0:T(8,128)(2,1)S(1)}, bf16[896,1024]{1,0:T(8,128)(2,1)S(1)}, u32[]{:S(2)}, u32[]{:S(2)}) %collective-permute-start.17) | collective-permute-done | bytes 1835040 | tf_op jit(solution)/shard_map/ppermute | solution.py:244
  1107.8 24.2 %multiply_convert_fusion.2 = bf16[640,2560]{1,0:T(8,128)(2,1)} fusion(f32[640,2560]{1,0:T(8,128)} %fusion.86, bf16[4096,12288]{1,0:T(8,128)(2,1)} %wu_ref.1, bf16[896,2560]{1,0:T(8,128)(2,1)} %collective-permute-done.23, bf16[896,2560]{1,0:T(8,128)(2,1)} %collective-permute-done.22, bf16[1024,4096]{1,0:T(8,128)(2,1)} %constant_dynamic-update-slice_fusion.10), kind=kOutput, calls=%fused_computation.123 | convolution fusion | flops 13438156800 | bytes 42598400 | tf_op jit(solution)/shard_map/dot_general | solution.py:229
  1156.5 267.3 %collective-permute-done.18 = bf16[896,4352]{1,0:T(8,128)(2,1)} collective-permute-done((bf16[896,4352]{1,0:T(8,128)(2,1)}, bf16[896,4352]{1,0:T(8,128)(2,1)}, u32[]{:S(2)}, u32[]{:S(2)}) %collective-permute-start.18) | collective-permute-done | bytes 7798816 | tf_op jit(solution)/shard_map/ppermute | solution.py:244
  1443.8 147.1 %collective-permute-done.19 = bf16[896,4352]{1,0:T(8,128)(2,1)} collective-permute-done((bf16[896,4352]{1,0:T(8,128)(2,1)}, bf16[896,4352]{1,0:T(8,128)(2,1)}, u32[]{:S(2)}, u32[]{:S(2)}) %collective-permute-start.19) | collective-permute-done | bytes 7798816 | tf_op jit(solution)/shard_map/ppermute | solution.py:244
  1650.6 37.4 %multiply_convert_fusion = bf16[640,4352]{1,0:T(8,128)(2,1)} fusion(f32[640,4352]{1,0:T(8,128)} %fusion.26, bf16[4096,12288]{1,0:T(8,128)(2,1)} %wu_ref.1, bf16[896,4352]{1,0:T(8,128)(2,1)} %collective-permute-done.21, bf16[896,4352]{1,0:T(8,128)(2,1)} %collective-permute-done.20, bf16[1024,4096]{1,0:T(8,128)(2,1)} %constant_dynamic-update-slice_fusion.10), kind=kOutput, calls=%fused_computation.106 | convolution fusion | flops 22844866560 | bytes 68747264 | tf_op jit(solution)/shard_map/dot_general | solution.py:229
  1688.0 37.5 %multiply_convert_fusion.1 = bf16[640,4352]{1,0:T(8,128)(2,1)} fusion(f32[640,4352]{1,0:T(8,128)} %fusion.38, bf16[4096,12288]{1,0:T(8,128)(2,1)} %wu_ref.1, bf16[896,4352]{1,0:T(8,128)(2,1)} %collective-permute-done.19, bf16[896,4352]{1,0:T(8,128)(2,1)} %collective-permute-done.18, bf16[1024,4096]{1,0:T(8,128)(2,1)} %constant_dynamic-update-slice_fusion.10), kind=kOutput, calls=%fused_computation.107 | convolution fusion | flops 22844866560 | bytes 68747264 | tf_op jit(solution)/shard_map/dot_general | solution.py:229
  1725.5 149.0 %fusion.40 = f32[1024,4096]{1,0:T(8,128)} fusion(bf16[12288,4096]{1,0:T(8,128)(2,1)} %w_ref.1, bf16[256,2560]{1,0:T(8,128)(2,1)} %multiply_convert_fusion.5, bf16[256,4352]{1,0:T(8,128)(2,1)} %multiply_convert_fusion.3, bf16[256,4352]{1,0:T(8,128)(2,1)} %multiply_convert_fusion.4, bf16[256,1024]{1,0:T(8,128)(2,1)} %copy-done.16, ...), kind=kOutput, calls=%fused_computation.40 | convolution fusion | flops 103305707520 | bytes 142606336 | tf_op jit(solution)/shard_map/dot_general | solution.py:229
  1883.1 21.5 fusion.72
  1904.6 23.5 collective-permute-done.26
  1929.8 43.9 %collective-permute-done.25 = bf16[1024,1024]{1,0:T(8,128)(2,1)S(1)} collective-permute-done((bf16[1024,1024]{1,0:T(8,128)(2,1)}, bf16[1024,1024]{1,0:T(8,128)(2,1)S(1)}, u32[]{:S(2)}, u32[]{:S(2)}) %collective-permute-start.25) | collective-permute-done | bytes 2097184 | tf_op jit(solution)/shard_map/ppermute | solution.py:251
  2001.7 216.3 %collective-permute-done.37 = bf16[256,4352]{1,0:T(8,128)(2,1)} collective-permute-done((bf16[256,4352]{1,0:T(8,128)(2,1)}, bf16[256,4352]{1,0:T(8,128)(2,1)}, u32[]{:S(2)}, u32[]{:S(2)}) %collective-permute-start.37) | collective-permute-done | bytes 2228256 | tf_op jit(solution)/shard_map/ppermute | solution.py:244
  2236.1 30.3 %fusion.6 = f32[640,4096]{1,0:T(8,128)} fusion(bf16[640,4352]{1,0:T(8,128)(2,1)} %collective-permute-done.29, bf16[12288,4096]{1,0:T(8,128)(2,1)} %w_ref.1), kind=kOutput, calls=%fused_computation.6 | convolution fusion | flops 22817013760 | bytes 51707904 | tf_op jit(solution)/shard_map/dot_general | solution.py:229
  2266.4 30.3 %fusion.2 = f32[640,4096]{1,0:T(8,128)} fusion(bf16[640,4352]{1,0:T(8,128)(2,1)} %collective-permute-done.30, bf16[12288,4096]{1,0:T(8,128)(2,1)} %w_ref.1), kind=kOutput, calls=%fused_computation.2 | convolution fusion | flops 22817013760 | bytes 51707904 | tf_op jit(solution)/shard_map/dot_general | solution.py:229
  2349.6 27.0 %collective-permute-done.32 = bf16[640,1024]{1,0:T(8,128)(2,1)} collective-permute-done((bf16[640,1024]{1,0:T(8,128)(2,1)}, bf16[640,1024]{1,0:T(8,128)(2,1)}, u32[]{:S(2)}, u32[]{:S(2)}) %collective-permute-start.32) | collective-permute-done | bytes 1310752 | tf_op jit(solution)/shard_map/ppermute | solution.py:251
  (197 shorter events, 665.2 us)
Async XLA Ops:
  13.5 99.2 %collective-permute-start.13 = (bf16[896,1024]{1,0:T(8,128)(2,1)}, bf16[896,1024]{1,0:T(8,128)(2,1)}, u32[]{:S(2)}, u32[]{:S(2)}) collective-permute-start(bf16[896,1024]{1,0:T(8,128)(2,1)} %get-tuple-element.32), channel_id=1, source_target_pairs={{0,1},{1,2},{2,3},{3,0},{4,5},{5,6},{6,7},{7,4}} | collective-permute-start | bytes 5505032 | tf_op jit(solution)/shard_map/ppermute | solution.py:251
  14.1 101.8 %collective-permute-start.14 = (bf16[896,1024]{1,0:T(8,128)(2,1)}, bf16[896,1024]{1,0:T(8,128)(2,1)}, u32[]{:S(2)}, u32[]{:S(2)}) collective-permute-start(bf16[896,1024]{1,0:T(8,128)(2,1)} %get-tuple-element.32), channel_id=1, source_target_pairs={{0,2},{1,3},{2,0},{3,1},{4,6},{5,7},{6,4},{7,5}} | collective-permute-start | bytes 5505032 | tf_op jit(solution)/shard_map/ppermute | solution.py:251
  15.2 103.8 %collective-permute-start.15 = (bf16[896,1024]{1,0:T(8,128)(2,1)}, bf16[896,1024]{1,0:T(8,128)(2,1)}, u32[]{:S(2)}, u32[]{:S(2)}) collective-permute-start(bf16[896,1024]{1,0:T(8,128)(2,1)} %get-tuple-element.32), channel_id=1, source_target_pairs={{0,3},{1,0},{2,1},{3,2},{4,7},{5,4},{6,5},{7,6}} | collective-permute-start | bytes 5505032 | tf_op jit(solution)/shard_map/ppermute | solution.py:251
  15.8 330.6 %collective-permute-start = (bf16[1024,1024]{1,0:T(8,128)(2,1)}, bf16[1024,1024]{1,0:T(8,128)(2,1)}, u32[]{:S(2)}, u32[]{:S(2)}) collective-permute-start(bf16[1024,1024]{1,0:T(8,128)(2,1)} %get-tuple-element.23), channel_id=1, source_target_pairs={{0,1},{1,2},{2,3},{3,0},{4,5},{5,6},{6,7},{7,4}} | collective-permute-start | bytes 6291464 | tf_op jit(solution)/shard_map/ppermute | solution.py:251
  15.8 335.1 %collective-permute-start.1 = (bf16[1024,1024]{1,0:T(8,128)(2,1)}, bf16[1024,1024]{1,0:T(8,128)(2,1)}, u32[]{:S(2)}, u32[]{:S(2)}) collective-permute-start(bf16[1024,1024]{1,0:T(8,128)(2,1)} %get-tuple-element.23), channel_id=1, source_target_pairs={{0,2},{1,3},{2,0},{3,1},{4,6},{5,7},{6,4},{7,5}} | collective-permute-start | bytes 6291464 | tf_op jit(solution)/shard_map/ppermute | solution.py:251
  112.7 242.1 %collective-permute-start.2 = (bf16[1024,1024]{1,0:T(8,128)(2,1)}, bf16[1024,1024]{1,0:T(8,128)(2,1)}, u32[]{:S(2)}, u32[]{:S(2)}) collective-permute-start(bf16[1024,1024]{1,0:T(8,128)(2,1)} %get-tuple-element.23), channel_id=1, source_target_pairs={{0,3},{1,0},{2,1},{3,2},{4,7},{5,4},{6,5},{7,6}} | collective-permute-start | bytes 6291464 | tf_op jit(solution)/shard_map/ppermute | solution.py:251
  115.9 428.3 %collective-permute-start.3 = (bf16[128,1024]{1,0:T(8,128)(2,1)}, bf16[128,1024]{1,0:T(8,128)(2,1)}, u32[]{:S(2)}, u32[]{:S(2)}) collective-permute-start(bf16[128,1024]{1,0:T(8,128)(2,1)} %get-tuple-element.24), channel_id=1, source_target_pairs={{0,4},{4,0},{1,5},{5,1},{2,6},{6,2},{3,7},{7,3}} | collective-permute-start | bytes 786440 | tf_op jit(solution)/shard_map/ppermute | solution.py:244
  119.0 431.5 %collective-permute-start.4 = (bf16[128,1024]{1,0:T(8,128)(2,1)}, bf16[128,1024]{1,0:T(8,128)(2,1)}, u32[]{:S(2)}, u32[]{:S(2)}) collective-permute-start(bf16[128,1024]{1,0:T(8,128)(2,1)} %get-tuple-element.25), channel_id=1, source_target_pairs={{0,4},{4,0},{1,5},{5,1},{2,6},{6,2},{3,7},{7,3}} | collective-permute-start | bytes 786440 | tf_op jit(solution)/shard_map/ppermute | solution.py:244
  346.4 159.4 %collective-permute-start.5 = (bf16[128,2048]{1,0:T(8,128)(2,1)}, bf16[128,2048]{1,0:T(8,128)(2,1)}, u32[]{:S(2)}, u32[]{:S(2)}) collective-permute-start(bf16[128,2048]{1,0:T(8,128)(2,1)} %fusion.215), channel_id=1, source_target_pairs={{0,4},{4,0},{1,5},{5,1},{2,6},{6,2},{3,7},{7,3}} | collective-permute-start | bytes 1572872 | tf_op jit(solution)/shard_map/ppermute | solution.py:244
  350.9 164.9 %collective-permute-start.6 = (bf16[128,2048]{1,0:T(8,128)(2,1)}, bf16[128,2048]{1,0:T(8,128)(2,1)}, u32[]{:S(2)}, u32[]{:S(2)}) collective-permute-start(bf16[128,2048]{1,0:T(8,128)(2,1)} %fusion.218), channel_id=1, source_target_pairs={{0,4},{4,0},{1,5},{5,1},{2,6},{6,2},{3,7},{7,3}} | collective-permute-start | bytes 1572872 | tf_op jit(solution)/shard_map/ppermute | solution.py:244
  525.5 581.6 %collective-permute-start.22 = (bf16[896,2560]{1,0:T(8,128)(2,1)}, bf16[896,2560]{1,0:T(8,128)(2,1)}, u32[]{:S(2)}, u32[]{:S(2)}) collective-permute-start(bf16[896,2560]{1,0:T(8,128)(2,1)} %fusion.156), channel_id=1, source_target_pairs={{0,4},{4,0},{1,5},{5,1},{2,6},{6,2},{3,7},{7,3}} | collective-permute-start | bytes 13762568 | tf_op jit(solution)/shard_map/ppermute | solution.py:244
  534.7 573.1 %collective-permute-start.23 = (bf16[896,2560]{1,0:T(8,128)(2,1)}, bf16[896,2560]{1,0:T(8,128)(2,1)}, u32[]{:S(2)}, u32[]{:S(2)}) collective-permute-start(bf16[896,2560]{1,0:T(8,128)(2,1)} %fusion.159), channel_id=1, source_target_pairs={{0,4},{4,0},{1,5},{5,1},{2,6},{6,2},{3,7},{7,3}} | collective-permute-start | bytes 13762568 | tf_op jit(solution)/shard_map/ppermute | solution.py:244
  544.2 1067.3 %collective-permute-start.20 = (bf16[896,4352]{1,0:T(8,128)(2,1)}, bf16[896,4352]{1,0:T(8,128)(2,1)}, u32[]{:S(2)}, u32[]{:S(2)}) collective-permute-start(bf16[896,4352]{1,0:T(8,128)(2,1)} %fusion.114), channel_id=1, source_target_pairs={{0,4},{4,0},{1,5},{5,1},{2,6},{6,2},{3,7},{7,3}} | collective-permute-start | bytes 23396360 | tf_op jit(solution)/shard_map/ppermute | solution.py:244
  550.5 450.0 %collective-permute-start.16 = (bf16[896,1024]{1,0:T(8,128)(2,1)}, bf16[896,1024]{1,0:T(8,128)(2,1)}, u32[]{:S(2)}, u32[]{:S(2)}) collective-permute-start(bf16[896,1024]{1,0:T(8,128)(2,1)} %fusion.231), channel_id=1, source_target_pairs={{0,4},{4,0},{1,5},{5,1},{2,6},{6,2},{3,7},{7,3}} | collective-permute-start | bytes 5505032 | tf_op jit(solution)/shard_map/ppermute | solution.py:244
  572.1 376.8 %collective-permute-start.45 = (bf16[128,1280]{1,0:T(8,128)(2,1)S(1)}, bf16[128,1280]{1,0:T(8,128)(2,1)S(1)}, u32[]{:S(2)}, u32[]{:S(2)}) collective-permute-start(bf16[128,1280]{1,0:T(8,128)(2,1)S(1)} %slice.244), channel_id=1, source_target_pairs={{0,4},{4,0},{1,5},{5,1},{2,6},{6,2},{3,7},{7,3}} | collective-permute-start | bytes 983048 | tf_op jit(solution)/shard_map/ppermute | solution.py:244
  1085.7 545.1 %collective-permute-start.21 = (bf16[896,4352]{1,0:T(8,128)(2,1)}, bf16[896,4352]{1,0:T(8,128)(2,1)}, u32[]{:S(2)}, u32[]{:S(2)}) collective-permute-start(bf16[896,4352]{1,0:T(8,128)(2,1)} %fusion.117), channel_id=1, source_target_pairs={{0,4},{4,0},{1,5},{5,1},{2,6},{6,2},{3,7},{7,3}} | collective-permute-start | bytes 23396360 | tf_op jit(solution)/shard_map/ppermute | solution.py:244
  1094.1 329.8 %collective-permute-start.18 = (bf16[896,4352]{1,0:T(8,128)(2,1)}, bf16[896,4352]{1,0:T(8,128)(2,1)}, u32[]{:S(2)}, u32[]{:S(2)}) collective-permute-start(bf16[896,4352]{1,0:T(8,128)(2,1)} %fusion.108), channel_id=1, source_target_pairs={{0,4},{4,0},{1,5},{5,1},{2,6},{6,2},{3,7},{7,3}} | collective-permute-start | bytes 23396360 | tf_op jit(solution)/shard_map/ppermute | solution.py:244
  1107.1 483.9 %collective-permute-start.19 = (bf16[896,4352]{1,0:T(8,128)(2,1)}, bf16[896,4352]{1,0:T(8,128)(2,1)}, u32[]{:S(2)}, u32[]{:S(2)}) collective-permute-start(bf16[896,4352]{1,0:T(8,128)(2,1)} %fusion.111), channel_id=1, source_target_pairs={{0,4},{4,0},{1,5},{5,1},{2,6},{6,2},{3,7},{7,3}} | collective-permute-start | bytes 23396360 | tf_op jit(solution)/shard_map/ppermute | solution.py:244
  1131.9 751.0 %collective-permute-start.27 = (bf16[640,2560]{1,0:T(8,128)(2,1)}, bf16[640,2560]{1,0:T(8,128)(2,1)}, u32[]{:S(2)}, u32[]{:S(2)}) collective-permute-start(bf16[640,2560]{1,0:T(8,128)(2,1)} %multiply_convert_fusion.2), channel_id=1, source_target_pairs={{0,4},{4,0},{1,5},{5,1},{2,6},{6,2},{3,7},{7,3}} | collective-permute-start | bytes 9830408 | tf_op jit(solution)/shard_map/ppermute | solution.py:244
  1423.8 895.1 %collective-permute-start.34 = (bf16[256,2560]{1,0:T(8,128)(2,1)}, bf16[256,2560]{1,0:T(8,128)(2,1)}, u32[]{:S(2)}, u32[]{:S(2)}) collective-permute-start(bf16[256,2560]{1,0:T(8,128)(2,1)} %multiply_convert_fusion.5), channel_id=1, source_target_pairs={{0,4},{4,0},{1,5},{5,1},{2,6},{6,2},{3,7},{7,3}} | collective-permute-start | bytes 3932168 | tf_op jit(solution)/shard_map/ppermute | solution.py:244
  1610.8 373.0 %collective-permute-start.36 = (bf16[256,4352]{1,0:T(8,128)(2,1)}, bf16[256,4352]{1,0:T(8,128)(2,1)}, u32[]{:S(2)}, u32[]{:S(2)}) collective-permute-start(bf16[256,4352]{1,0:T(8,128)(2,1)} %multiply_convert_fusion.4), channel_id=1, source_target_pairs={{0,4},{4,0},{1,5},{5,1},{2,6},{6,2},{3,7},{7,3}} | collective-permute-start | bytes 6684680 | tf_op jit(solution)/shard_map/ppermute | solution.py:244
  1928.2 307.9 %collective-permute-start.29 = (bf16[640,4352]{1,0:T(8,128)(2,1)}, bf16[640,4352]{1,0:T(8,128)(2,1)}, u32[]{:S(2)}, u32[]{:S(2)}) collective-permute-start(bf16[640,4352]{1,0:T(8,128)(2,1)} %multiply_convert_fusion.1), channel_id=1, source_target_pairs={{0,4},{4,0},{1,5},{5,1},{2,6},{6,2},{3,7},{7,3}} | collective-permute-start | bytes 16711688 | tf_op jit(solution)/shard_map/ppermute | solution.py:244
  1973.7 292.7 %collective-permute-start.30 = (bf16[640,4352]{1,0:T(8,128)(2,1)}, bf16[640,4352]{1,0:T(8,128)(2,1)}, u32[]{:S(2)}, u32[]{:S(2)}) collective-permute-start(bf16[640,4352]{1,0:T(8,128)(2,1)} %multiply_convert_fusion), channel_id=1, source_target_pairs={{0,4},{4,0},{1,5},{5,1},{2,6},{6,2},{3,7},{7,3}} | collective-permute-start | bytes 16711688 | tf_op jit(solution)/shard_map/ppermute | solution.py:244
  1974.6 243.4 %collective-permute-start.37 = (bf16[256,4352]{1,0:T(8,128)(2,1)}, bf16[256,4352]{1,0:T(8,128)(2,1)}, u32[]{:S(2)}, u32[]{:S(2)}) collective-permute-start(bf16[256,4352]{1,0:T(8,128)(2,1)} %multiply_convert_fusion.3), channel_id=1, source_target_pairs={{0,4},{4,0},{1,5},{5,1},{2,6},{6,2},{3,7},{7,3}} | collective-permute-start | bytes 6684680 | tf_op jit(solution)/shard_map/ppermute | solution.py:244
  (40 other events, 1634.4 us)
